TPU v7x, 512 devices: a whole 4x8x8 slice. The times are simulated.
512 devices in a mesh: expert: 32 (over z, y_hi, core), ctx: 16 (over x, y_lo).
Axes of the slice: x: 4, y: 8 (y_hi: 2, y_lo: 4; y = y_hi * 4 + y_lo), z: 8, core: 2. Of those that a mesh axis runs over, the one named last changes fastest.
Arguments:
- query_latent: bfloat16 [4096, 128, 512], P('ctx', 'expert'), may hold values from -3 to 3
- query_rope: bfloat16 [4096, 8192], P('ctx', 'expert'), may hold values from -128 to 128
- latent_cache: bfloat16 [576, 4096], P(None, 'ctx'), may hold values from -32 to 32
- group_order: int32 [16], replicated, may hold values from 0 to 15, each once
Outputs:
- attention_out: bfloat16 [4096, 128, 512], P('ctx', 'expert')
Inputs may be any that keep to these rules, and one draw needn't show every extreme that they name: `group_order`: each block index appears once.
All inputs are finite; a program needn't handle non-finite values.
Results may differ from a plain program's by a relative error of at most 0.0045.
Values may be sent and summed in bfloat16 or wider, within the bound.
No kernel may reach another device: no remote copies, remote signals or barrier semaphores. Data moves between devices by JAX's collectives and lax.ppermute only.
A program may use at most 64 MiB of HBM per device.

v0:
```python
import functools
import math

import jax
import jax.numpy as jnp
from jax import lax
from jax.experimental import pallas as pl
from jax.experimental.pallas import tpu as pltpu
from jax.sharding import Mesh
from jax.sharding import PartitionSpec as P


LOG_SCALE = 192.0 ** (-0.5) * math.log2(math.e)
MASKED = -1e30
FLOOR = -1e29
RING = ("yh", "co", "x", "yl")
HALF = 128
VMEM_MIB = 16
QUERY = 640
USED = 576
OUTER = (-1, 1, 2)
WIDTH = 512
STATE = 768
PEAK = slice(512, 640)
TOTAL = slice(640, 768)
f32 = jnp.float32


def split_permute(value, shift, along):
    pairs = []
    for y in range(8):
        for core in range(2):
            for x in range(4):
                to_y, to_x = y, x
                if (core == 0) == (along == 0):
                    step = shift
                    if shift == 2 and y % 2:
                        step = -2
                    to_y = (y + step) % 8
                else:
                    to_x = (x + shift) % 4
                at = lambda u, v: (((u // 4) * 2 + core) * 4 + v) * 4 + u % 4
                pairs.append((at(y, x), at(to_y, to_x)))
    return lax.ppermute(value, RING, pairs)


def near_groups():
    groups = []
    for half in range(2):
        at = lambda core, x, y: ((half * 2 + core) * 4 + x) * 4 + y
        groups += [[at(0, x, y) for y in range(4)] for x in range(4)]
        groups += [[at(1, x, y) for x in range(4)] for y in range(4)]
    return groups


def keys_of(refs):
    tiles = [ref[i] for ref in refs for i in range(ref.shape[0])]
    return jnp.concatenate(tiles, axis=1)


def scores_of(queries, keys):
    return jnp.dot(queries[:, :USED], keys, preferred_element_type=f32)


def mix(weights, keys):
    return lax.dot_general(
        weights, keys[:WIDTH], (((1,), (1,)), ((), ())), preferred_element_type=f32
    )


def soften(parts, peak, total):
    top = parts[0]
    for part in parts[1:]:
        top = jnp.maximum(top, part)
    row_top = jnp.max(top, axis=1, keepdims=True)
    new_peak = jnp.maximum(peak, jnp.broadcast_to(row_top, top.shape))
    offset = new_peak * LOG_SCALE
    weights = [jnp.exp2(part * LOG_SCALE - offset) for part in parts]
    keep = jnp.exp2(peak * LOG_SCALE - offset)
    added = weights[0]
    for part in weights[1:]:
        added = added + part
    total = added if total is None else total * keep + added
    return jnp.concatenate([w.astype(jnp.bfloat16) for w in weights], axis=1), new_peak, total, keep


def pieces_of(scores):
    return [scores[:, i : i + HALF] for i in range(0, scores.shape[1], HALF)]


def block_of(place, inner, outer):
    core, x, y = place
    at_y = jnp.where(core == 0, inner, (y + outer + 4) % 4)
    at_x = jnp.where(core == 0, (x + outer + 4) % 4, inner)
    return at_x * 4 + at_y


def here(place_ref):
    return place_ref[0], place_ref[1], place_ref[2]


def masked_pieces(scores, order_ref, place_ref, parts):
    place = here(place_ref)
    mine = order_ref[place[1] * 4 + place[2]]
    pieces = pieces_of(scores)
    for i, part in enumerate(pieces):
        block = block_of(place, i % 4, OUTER[parts[i // 4]])
        pieces[i] = jnp.where(order_ref[block] < mine, part, MASKED)
    return pieces


def scaled(numer, factor):
    return jnp.concatenate([part * factor for part in pieces_of(numer)], axis=1)


def put_state(ref, h, numer, peak, total):
    ref[h, :, :WIDTH] = numer
    ref[h, :, PEAK] = peak
    ref[h, :, TOTAL] = total


def near_kernel(order_ref, place_ref, q_ref, kv_ref, out, *keep):
    for ref in keep:
        ref[...] = q_ref[...]
    keys = keys_of([kv_ref])
    rows = q_ref.shape[1]
    lane = lax.broadcasted_iota(jnp.int32, (rows, HALF), 1)
    place = here(place_ref)
    mine = order_ref[place[1] * 4 + place[2]]
    limits = []
    for i in range(4):
        order = order_ref[block_of(place, i, 0)]
        limit = jnp.where(order < mine, 4096, -4096)
        limits.append(jnp.where(order == mine, -HALF * place[0], limit))
    ahead_by = lane - lax.broadcasted_iota(jnp.int32, (rows, HALF), 0)
    scores = scores_of(q_ref[0], keys)
    for h in range(4):
        ahead = scores_of(q_ref[h + 1], keys) if h < 3 else None
        parts = [
            jnp.where(ahead_by <= limit, part, MASKED)
            for limit, part in zip(limits, pieces_of(scores))
        ]
        floor = jnp.full((rows, HALF), FLOOR, f32)
        weights, peak, total, _ = soften(parts, floor, None)
        put_state(out, h, mix(weights, keys), peak, total)
        scores = ahead


def more_kernel(parts_in, order_ref, place_ref, q_ref, state_ref, *refs):
    keys = keys_of(refs[:-1])
    out = refs[-1]
    scores = scores_of(q_ref[0], keys)
    for h in range(4):
        ahead = scores_of(q_ref[h + 1], keys) if h < 3 else None
        parts = masked_pieces(scores, order_ref, place_ref, parts_in)
        weights, peak, total, keep = soften(parts, state_ref[h, :, PEAK], state_ref[h, :, TOTAL])
        numer = scaled(state_ref[h, :, :WIDTH], keep) + mix(weights, keys)
        put_state(out, h, numer, peak, total)
        scores = ahead


def last_kernel(parts_in, order_ref, place_ref, q_ref, state_ref, other_ref, kv_ref, out):
    keys = keys_of([kv_ref])
    scores = scores_of(q_ref[0], keys)
    for h in range(4):
        ahead = scores_of(q_ref[h + 1], keys) if h < 3 else None
        parts = masked_pieces(scores, order_ref, place_ref, parts_in)
        peak, other_peak = state_ref[h, :, PEAK], other_ref[h, :, PEAK]
        floor = jnp.maximum(peak, other_peak)
        weights, top, added, _ = soften(parts, floor, None)
        mine = jnp.exp2((peak - top) * LOG_SCALE)
        theirs = jnp.exp2((other_peak - top) * LOG_SCALE)
        total = state_ref[h, :, TOTAL] * mine + other_ref[h, :, TOTAL] * theirs + added
        share = 1.0 / jnp.sum(total, axis=1, keepdims=True)
        numer = scaled(state_ref[h, :, :WIDTH], mine) + scaled(other_ref[h, :, :WIDTH], theirs)
        numer = numer + mix(weights, keys)
        out[:, h, :] = (numer * share).astype(jnp.bfloat16)
        scores = ahead


def prepare_kernel(latent_ref, rope_ref, out):
    for h in range(4):
        out[h, :, :WIDTH] = latent_ref[:, h, :]
        rope = rope_ref[:, h * 64 : h * 64 + 64]
        out[h, :, WIDTH:] = jnp.concatenate([rope, jnp.zeros_like(rope)], axis=1)


def prepare(latent, rope):
    rows, heads, _ = latent.shape
    return pl.pallas_call(
        prepare_kernel,
        grid=(4,),
        out_shape=jax.ShapeDtypeStruct((heads, rows, QUERY), jnp.bfloat16),
        in_specs=[
            pl.BlockSpec((rows // 4, heads, WIDTH), lambda i: (i, 0, 0)),
            pl.BlockSpec((rows // 4, heads * 64), lambda i: (i, 0)),
        ],
        out_specs=pl.BlockSpec((heads, rows // 4, QUERY), lambda i: (0, i, 0)),
        compiler_params=pltpu.CompilerParams(vmem_limit_bytes=VMEM_MIB * 2**20),
        cost_estimate=pl.CostEstimate(flops=1 << 30, bytes_accessed=2_000_000, transcendentals=0),
        name="prepare",
    )(latent, rope)


def spread_kernel(place_ref, cache_ref, out):
    for i in range(4):
        out[i] = cache_ref[...]


def spread(cache, place):
    rows = cache.shape[0]
    copies = pl.pallas_call(
        spread_kernel,
        grid_spec=pltpu.PrefetchScalarGridSpec(
            num_scalar_prefetch=1,
            grid=(1,),
            in_specs=[pl.BlockSpec((rows, HALF), lambda i, place: (0, place[0]))],
            out_specs=pl.BlockSpec((4, rows, HALF), lambda i, place: (0, 0, 0)),
        ),
        out_shape=jax.ShapeDtypeStruct((4, rows, HALF), cache.dtype),
        compiler_params=pltpu.CompilerParams(vmem_limit_bytes=VMEM_MIB * 2**20),
        name="spread",
    )(place, cache)
    return copies.reshape(4 * rows, HALF)


VM = pl.BlockSpec(memory_space=pltpu.VMEM)
SM = pl.BlockSpec(memory_space=pltpu.SMEM)


def call(kernel, out_shape, pieces, where, args, aliases=None):
    heads, keys = 4, pieces * HALF
    cost = pl.CostEstimate(
        flops=2 * heads * 256 * keys * (WIDTH * 2 + 64) * 2,
        bytes_accessed=4_000_000,
        transcendentals=heads * 256 * keys,
    )
    args = [*where, *args]
    specs = [SM] * len(where) + [VM] * (len(args) - len(where))
    return pl.pallas_call(
        kernel,
        out_shape=out_shape,
        in_specs=specs,
        out_specs=[VM] * len(out_shape) if isinstance(out_shape, list) else VM,
        input_output_aliases=aliases or {},
        compiler_params=pltpu.CompilerParams(vmem_limit_bytes=VMEM_MIB * 2**20),
        cost_estimate=cost,
    )(*args)


def attend(query_latent, query_rope, latent_cache, group_order):
    rows, heads, _ = query_latent.shape
    core = lax.axis_index("co")
    x, y = lax.axis_index("x"), lax.axis_index("yl")
    where = [group_order, jnp.stack([core, x, y]).astype(jnp.int32)]
    copies = spread(latent_cache, where[1])
    bundle = lax.all_to_all(copies, RING, 0, 0, axis_index_groups=near_groups(), tiled=True)
    queries = prepare(query_latent, query_rope)
    bundle = bundle.reshape(4, WIDTH + 64, HALF)
    far = []
    for shift in (1, -1, 2):
        far.append(split_permute(bundle, shift, 1))
    twin = lax.ppermute(queries, "co", [(0, 1), (1, 0)])

    state = jax.ShapeDtypeStruct((heads, rows, STATE), f32)

    def more(queries, state_in, *parts):
        kernel = functools.partial(more_kernel, parts)
        args = [queries, state_in, *(far[part] for part in parts)]
        return call(kernel, state, 4 * len(parts), where, args, {3: 0})

    own = call(near_kernel, state, 4, where, [queries, bundle])
    packed = jax.ShapeDtypeStruct(twin.shape, twin.dtype)
    sib, twin = call(near_kernel, [state, packed], 4, where, [twin, bundle])
    sib = more(twin, sib, 0)
    sib = more(twin, sib, 1, 2)
    other = lax.ppermute(sib, "co", [(0, 1), (1, 0)])
    own = more(queries, own, 0, 1)
    out = jax.ShapeDtypeStruct((rows, heads, WIDTH), jnp.bfloat16)
    last = functools.partial(last_kernel, (2,))
    return call(last, out, 4, where, [queries, own, other, far[2]])


def solution(mesh):
    depth = mesh.shape["expert"] // 4
    torus = Mesh(mesh.devices.reshape(depth, 2, 2, 4, 4), ("z",) + RING)
    expert, ctx = ("z", "yh", "co"), ("x", "yl")
    placed = (P(ctx, expert, None), P(ctx, expert), P(None, ctx), P())
    return jax.shard_map(
        attend, mesh=torus, in_specs=placed, out_specs=P(ctx, expert, None), check_vma=False
    )
```

profile of v0, /device:TPU:1, one launch (start us, length us, event | category | flops | bytes accessed | tf_op | source)
XLA Modules:
  0.0 65.7 jit_solution(3461768943840997639)
XLA Ops:
  0.0 0.0 copy-start
  0.0 0.0 copy-start.2
  0.0 1.3 %copy-done.2 = bf16[256,4,512]{2,1,0:T(4,128)(2,1)S(1)} copy-done((bf16[256,4,512]{2,1,0:T(4,128)(2,1)S(1)}, bf16[256,4,512]{2,1,0:T(4,128)(2,1)}, u32[]{:S(2)}) %copy-start.2) | copy-done | bytes 1048600
  1.3 0.0 copy-start.3
  1.3 0.9 %copy-done.3 = bf16[256,256]{1,0:T(8,128)(2,1)S(1)} copy-done((bf16[256,256]{1,0:T(8,128)(2,1)S(1)}, bf16[256,256]{1,0:T(8,128)(2,1)}, u32[]{:S(2)}) %copy-start.3) | copy-done | bytes 131096
  2.2 0.0 copy-start.1
  2.2 2.3 %prepare.1.q_ref = bf16[4,256,640]{2,1,0:T(8,128)(2,1)S(1)} custom-call(bf16[256,4,512]{2,1,0:T(4,128)(2,1)S(1)} %copy-done.2, bf16[256,256]{1,0:T(8,128)(2,1)S(1)} %copy-done.3), custom_call_target="tpu_custom_call" | custom-call | flops 1073741824 | bytes 2000000 | tf_op jit(solution)/shard_map/prepare/pallas_call | solution.py:190
  4.5 8.7 %collective-permute-start.2 = (bf16[4,256,640]{2,1,0:T(8,128)(2,1)S(1)}, bf16[4,256,640]{2,1,0:T(8,128)(2,1)S(1)}, u32[]{:S(2)}, u32[]{:S(2)}) collective-permute-start(bf16[4,256,640]{2,1,0:T(8,128)(2,1)S(1)} %prepare.1.q_ref), channel_id=1, source_target_pairs={{0,16},{16,0},{1,17},{17,1},{2,18},{18,2},{3,19},{19,3},{4,20},{20... | collective-permute-start | bytes 3932168 | tf_op jit(solution)/shard_map/ppermute | solution.py:263
  13.2 0.1 pad_add_fusion.place_ref
  13.3 0.0 copy-done
  13.3 0.6 spread.1
  14.0 9.8 %all_to_all.6.kv_ref = bf16[4,576,128]{2,1,0:T(8,128)(2,1)S(1)} all-to-all(bf16[4,576,128]{2,1,0:T(8,128)(2,1)S(1)} %spread.1), channel_id=1, replica_groups={{0,1,2,3},{4,5,6,7},{8,9,10,11},{12,13,14,15},{16,20,24,28},{17,21,25,2..., dimensions={0} | all-to-all | bytes 1179648 | tf_op jit(solution)/shard_map/all_to_all | solution.py:257
  23.8 1.9 %collective-permute-start = (bf16[4,576,128]{2,1,0:T(8,128)(2,1)S(1)}, bf16[4,576,128]{2,1,0:T(8,128)(2,1)S(1)}, u32[]{:S(2)}, u32[]{:S(2)}) collective-permute-start(bf16[4,576,128]{2,1,0:T(8,128)(2,1)S(1)} %all_to_all.6.kv_ref), channel_id=1, source_target_pairs={{0,4},{4,8},{8,12},{12,0},{16,17},{20,21},{24,25},{28,29},{1,5},{5... | collective-permute-start | bytes 1769480 | tf_op jit(solution)/shard_map/ppermute | solution.py:44
  25.7 4.6 %collective-permute-start.1 = (bf16[4,576,128]{2,1,0:T(8,128)(2,1)S(1)}, bf16[4,576,128]{2,1,0:T(8,128)(2,1)S(1)}, u32[]{:S(2)}, u32[]{:S(2)}) collective-permute-start(bf16[4,576,128]{2,1,0:T(8,128)(2,1)S(1)} %all_to_all.6.kv_ref), channel_id=1, source_target_pairs={{0,12},{4,0},{8,4},{12,8},{16,51},{20,55},{24,59},{28,63},{1,13},{... | collective-permute-start | bytes 1769480 | tf_op jit(solution)/shard_map/ppermute | solution.py:44
  30.3 1.9 %collective-permute-start.3 = (bf16[4,576,128]{2,1,0:T(8,128)(2,1)S(1)}, bf16[4,576,128]{2,1,0:T(8,128)(2,1)S(1)}, u32[]{:S(2)}, u32[]{:S(2)}) collective-permute-start(bf16[4,576,128]{2,1,0:T(8,128)(2,1)S(1)} %all_to_all.6.kv_ref), channel_id=1, source_target_pairs={{0,8},{4,12},{8,0},{12,4},{16,18},{20,22},{24,26},{28,30},{1,9},{5... | collective-permute-start | bytes 1769480 | tf_op jit(solution)/shard_map/ppermute | solution.py:44
  32.2 0.0 collective-permute-done.2.q_ref
  32.2 0.0 copy-done.1
  32.2 2.3 %shard_map.48 = (f32[4,256,768]{2,1,0:T(8,128)S(1)}, bf16[4,256,640]{2,1,0:T(8,128)(2,1)S(1)}) custom-call(s32[16]{0:T(128)S(1)} %copy-done.1, s32[3]{0:T(128)S(1)} %pad_add_fusion.place_ref, bf16[4,256,640]{2,1,0:T(8,128)(2,1)S(1)} %collective-permute-done.2.q_ref, bf16[4,576,128]{2,1,0:T(8,128)(2,1)S(1)} %all_to_all.6.kv_ref), custom_call_target="tpu_custom_call" | custom-call | flops 2281701376 | bytes 4000000 | tf_op jit(solution)/shard_map/pallas_call | solution.py:240
  34.5 1.4 %collective-permute-done.refs_0_ = bf16[4,576,128]{2,1,0:T(8,128)(2,1)S(1)} collective-permute-done((bf16[4,576,128]{2,1,0:T(8,128)(2,1)S(1)}, bf16[4,576,128]{2,1,0:T(8,128)(2,1)S(1)}, u32[]{:S(2)}, u32[]{:S(2)}) %collective-permute-start) | collective-permute-done | bytes 589856 | tf_op jit(solution)/shard_map/ppermute | solution.py:44
  35.9 2.7 %shard_map.49.state_ref = f32[4,256,768]{2,1,0:T(8,128)S(1)} custom-call(s32[16]{0:T(128)S(1)} %copy-done.1, s32[3]{0:T(128)S(1)} %pad_add_fusion.place_ref, bf16[4,256,640]{2,1,0:T(8,128)(2,1)S(1)} %get-tuple-element.7.q_ref, f32[4,256,768]{2,1,0:T(8,128)S(1)} %get-tuple-element.8.state_ref, ...), custom_call_target="tpu_custom_call", output_to_operand_aliasing={{}: (3, {})} | custom-call | flops 2281701376 | bytes 4000000 | tf_op jit(solution)/shard_map/pallas_call | solution.py:240
  38.6 4.8 %collective-permute-done.1.refs_1_.refs_0_ = bf16[4,576,128]{2,1,0:T(8,128)(2,1)S(1)} collective-permute-done((bf16[4,576,128]{2,1,0:T(8,128)(2,1)S(1)}, bf16[4,576,128]{2,1,0:T(8,128)(2,1)S(1)}, u32[]{:S(2)}, u32[]{:S(2)}) %collective-permute-start.1) | collective-permute-done | bytes 589856 | tf_op jit(solution)/shard_map/ppermute | solution.py:44
  43.4 0.0 collective-permute-done.3.refs_1_.kv_ref
  43.4 4.4 %shard_map.50 = f32[4,256,768]{2,1,0:T(8,128)S(1)} custom-call(s32[16]{0:T(128)S(1)} %copy-done.1, s32[3]{0:T(128)S(1)} %pad_add_fusion.place_ref, bf16[4,256,640]{2,1,0:T(8,128)(2,1)S(1)} %get-tuple-element.7.q_ref, f32[4,256,768]{2,1,0:T(8,128)S(1)} %shard_map.49.state_ref, ...), custom_call_target="tpu_custom_call", output_to_operand_aliasing={{}: (3, {})} | custom-call | flops 4563402752 | bytes 4000000 | tf_op jit(solution)/shard_map/pallas_call | solution.py:240
  47.8 6.8 %collective-permute-start.4 = (f32[4,256,768]{2,1,0:T(8,128)S(1)}, f32[4,256,768]{2,1,0:T(8,128)S(1)}, u32[]{:S(2)}, u32[]{:S(2)}) collective-permute-start(f32[4,256,768]{2,1,0:T(8,128)S(1)} %shard_map.50), channel_id=1, source_target_pairs={{0,16},{16,0},{1,17},{17,1},{2,18},{18,2},{3,19},{19,3},{4,20},{20... | collective-permute-start | bytes 9437192 | tf_op jit(solution)/shard_map/ppermute | solution.py:277
  54.6 2.1 %shard_map.46.state_ref = f32[4,256,768]{2,1,0:T(8,128)S(1)} custom-call(s32[16]{0:T(128)S(1)} %copy-done.1, s32[3]{0:T(128)S(1)} %pad_add_fusion.place_ref, bf16[4,256,640]{2,1,0:T(8,128)(2,1)S(1)} %prepare.1.q_ref, bf16[4,576,128]{2,1,0:T(8,128)(2,1)S(1)} %all_to_all.6.kv_ref), custom_call_target="tpu_custom_call" | custom-call | flops 2281701376 | bytes 4000000 | tf_op jit(solution)/shard_map/pallas_call | solution.py:240
  56.8 4.4 %shard_map.47.state_ref = f32[4,256,768]{2,1,0:T(8,128)S(1)} custom-call(s32[16]{0:T(128)S(1)} %copy-done.1, s32[3]{0:T(128)S(1)} %pad_add_fusion.place_ref, bf16[4,256,640]{2,1,0:T(8,128)(2,1)S(1)} %prepare.1.q_ref, f32[4,256,768]{2,1,0:T(8,128)S(1)} %shard_map.46.state_ref, ...), custom_call_target="tpu_custom_call", output_to_operand_aliasing={{}: (3, {})} | custom-call | flops 4563402752 | bytes 4000000 | tf_op jit(solution)/shard_map/pallas_call | solution.py:240
  61.2 0.0 collective-permute-done.4.other_ref
  61.2 4.5 %shard_map.51 = bf16[256,4,512]{2,1,0:T(4,128)(2,1)} custom-call(s32[16]{0:T(128)S(1)} %copy-done.1, s32[3]{0:T(128)S(1)} %pad_add_fusion.place_ref, bf16[4,256,640]{2,1,0:T(8,128)(2,1)S(1)} %prepare.1.q_ref, f32[4,256,768]{2,1,0:T(8,128)S(1)} %shard_map.47.state_ref, f32[4,256,768]{2,1,0:T(8,128)S(1)} %collective-permute-done.4.other_ref, ...), custom_call_target="tpu_custom_call" | custom-call | flops 2281701376 | bytes 4000000 | tf_op jit(solution)/shard_map/pallas_call | solution.py:240
Async XLA Ops:
  0.0 13.3 %copy-start = (bf16[576,256]{1,0:T(8,128)(2,1)S(1)}, bf16[576,256]{1,0:T(8,128)(2,1)}, u32[]{:S(2)}) copy-start(bf16[576,256]{1,0:T(8,128)(2,1)} %cache_ref.1) | copy-start | bytes 884740
  0.0 1.3 %copy-start.2 = (bf16[256,4,512]{2,1,0:T(4,128)(2,1)S(1)}, bf16[256,4,512]{2,1,0:T(4,128)(2,1)}, u32[]{:S(2)}) copy-start(bf16[256,4,512]{2,1,0:T(4,128)(2,1)} %latent_ref.1) | copy-start | bytes 3145732
  1.3 0.9 %copy-start.3 = (bf16[256,256]{1,0:T(8,128)(2,1)S(1)}, bf16[256,256]{1,0:T(8,128)(2,1)}, u32[]{:S(2)}) copy-start(bf16[256,256]{1,0:T(8,128)(2,1)} %rope_ref.1) | copy-start | bytes 393220
  2.2 30.0 %copy-start.1 = (s32[16]{0:T(128)S(1)}, s32[16]{0:T(128)}, u32[]{:S(2)}) copy-start(s32[16]{0:T(128)} %order_ref.11) | copy-start | bytes 196
  4.5 27.7 %collective-permute-start.2 = (bf16[4,256,640]{2,1,0:T(8,128)(2,1)S(1)}, bf16[4,256,640]{2,1,0:T(8,128)(2,1)S(1)}, u32[]{:S(2)}, u32[]{:S(2)}) collective-permute-start(bf16[4,256,640]{2,1,0:T(8,128)(2,1)S(1)} %prepare.1.q_ref), channel_id=1, source_target_pairs={{0,16},{16,0},{1,17},{17,1},{2,18},{18,2},{3,19},{19,3},{4,20},{20... | collective-permute-start | bytes 3932168 | tf_op jit(solution)/shard_map/ppermute | solution.py:263
  23.8 12.1 %collective-permute-start = (bf16[4,576,128]{2,1,0:T(8,128)(2,1)S(1)}, bf16[4,576,128]{2,1,0:T(8,128)(2,1)S(1)}, u32[]{:S(2)}, u32[]{:S(2)}) collective-permute-start(bf16[4,576,128]{2,1,0:T(8,128)(2,1)S(1)} %all_to_all.6.kv_ref), channel_id=1, source_target_pairs={{0,4},{4,8},{8,12},{12,0},{16,17},{20,21},{24,25},{28,29},{1,5},{5... | collective-permute-start | bytes 1769480 | tf_op jit(solution)/shard_map/ppermute | solution.py:44
  25.7 17.7 %collective-permute-start.1 = (bf16[4,576,128]{2,1,0:T(8,128)(2,1)S(1)}, bf16[4,576,128]{2,1,0:T(8,128)(2,1)S(1)}, u32[]{:S(2)}, u32[]{:S(2)}) collective-permute-start(bf16[4,576,128]{2,1,0:T(8,128)(2,1)S(1)} %all_to_all.6.kv_ref), channel_id=1, source_target_pairs={{0,12},{4,0},{8,4},{12,8},{16,51},{20,55},{24,59},{28,63},{1,13},{... | collective-permute-start | bytes 1769480 | tf_op jit(solution)/shard_map/ppermute | solution.py:44
  30.3 13.1 %collective-permute-start.3 = (bf16[4,576,128]{2,1,0:T(8,128)(2,1)S(1)}, bf16[4,576,128]{2,1,0:T(8,128)(2,1)S(1)}, u32[]{:S(2)}, u32[]{:S(2)}) collective-permute-start(bf16[4,576,128]{2,1,0:T(8,128)(2,1)S(1)} %all_to_all.6.kv_ref), channel_id=1, source_target_pairs={{0,8},{4,12},{8,0},{12,4},{16,18},{20,22},{24,26},{28,30},{1,9},{5... | collective-permute-start | bytes 1769480 | tf_op jit(solution)/shard_map/ppermute | solution.py:44
  47.8 13.4 %collective-permute-start.4 = (f32[4,256,768]{2,1,0:T(8,128)S(1)}, f32[4,256,768]{2,1,0:T(8,128)S(1)}, u32[]{:S(2)}, u32[]{:S(2)}) collective-permute-start(f32[4,256,768]{2,1,0:T(8,128)S(1)} %shard_map.50), channel_id=1, source_target_pairs={{0,16},{16,0},{1,17},{17,1},{2,18},{18,2},{3,19},{19,3},{4,20},{20... | collective-permute-start | bytes 9437192 | tf_op jit(solution)/shard_map/ppermute | solution.py:277
where the time goes:
time: 66.1 us; the launch traced here: 65.7 us
  starting transfers between devices  23.9 us (36%)
  Pallas kernels  23.4 us (35%)
  blocking collectives  9.81 us (15%)
  waiting for transfers between devices  6.2 us (9%)
  local copies, waits for them, and re-layouts  2.18 us (3%)
    pallas_call x6, Pallas kernels, call(): pl.pallas_call(kernel, out_shape=out_shape, in_specs=specs, out_specs=[VM...  20.4 us
    all_to_all x1, blocking collectives, attend(): lax.all_to_all(copies, RING, 0, 0, axis_index_groups=near_groups(), tiled...  9.81 us
    ppermute x1, starting transfers between devices, attend(): twin = lax.ppermute(queries, 'co', [(0, 1), (1, 0)])  8.75 us
    ppermute x3, starting transfers between devices, split_permute(): return lax.ppermute(value, RING, pairs)  8.4 us
    ppermute x1, starting transfers between devices, attend(): other = lax.ppermute(sib, 'co', [(0, 1), (1, 0)])  6.8 us
    ppermute x3, waiting for transfers between devices, split_permute(): return lax.ppermute(value, RING, pairs)  6.2 us
    pallas_call x1, Pallas kernels, prepare(): pl.pallas_call(prepare_kernel, grid=(4,), out_shape=jax.ShapeDtypeStruct(...  2.29 us
    unnamed x8, local copies, waits for them, and re-layouts  2.18 us
  transfers between devices with their start and end apart: 5, of which 2 were waited for; matrix products, arithmetic and copies ran while one was open for 0% of the time, Pallas kernels for 19%

commit v1 on v0

--- a/solution.py
+++ b/solution.py
@@ -24,6 +24,8 @@
 PEAK = slice(512, 640)
 TOTAL = slice(640, 768)
 f32 = jnp.float32
+VM = pl.BlockSpec(memory_space=pltpu.VMEM)
+SM = pl.BlockSpec(memory_space=pltpu.SMEM)
 
 
 def split_permute(value, shift, along):
@@ -95,17 +97,21 @@
     return at_x * 4 + at_y
 
 
-def here(place_ref):
-    return place_ref[0], place_ref[1], place_ref[2]
-
-
-def masked_pieces(scores, order_ref, place_ref, parts):
-    place = here(place_ref)
+def fill_seen(order_ref, place_ref, seen_ref):
+    place = place_ref[0], place_ref[1], place_ref[2]
     mine = order_ref[place[1] * 4 + place[2]]
+    for i in range(16):
+        order = order_ref[block_of(place, i % 4, (0, *OUTER)[i // 4])]
+        limit = jnp.where(order < mine, 4096, -4096)
+        limit = jnp.where(order == mine, -HALF * place[0], limit)
+        seen_ref[i : i + 1, :] = jnp.full((1, HALF), limit, jnp.int32)
+
+
+def masked_pieces(scores, seen_ref, parts):
     pieces = pieces_of(scores)
     for i, part in enumerate(pieces):
-        block = block_of(place, i % 4, OUTER[parts[i // 4]])
-        pieces[i] = jnp.where(order_ref[block] < mine, part, MASKED)
+        row = 4 + 4 * parts[i // 4] + i % 4
+        pieces[i] = jnp.where(seen_ref[row : row + 1, :] > 0, part, MASKED)
     return pieces
 
 
@@ -119,26 +125,19 @@
     ref[h, :, TOTAL] = total
 
 
-def near_kernel(order_ref, place_ref, q_ref, kv_ref, out, *keep):
+def near_kernel(seen_ref, q_ref, kv_ref, out, *keep):
     for ref in keep:
         ref[...] = q_ref[...]
     keys = keys_of([kv_ref])
     rows = q_ref.shape[1]
     lane = lax.broadcasted_iota(jnp.int32, (rows, HALF), 1)
-    place = here(place_ref)
-    mine = order_ref[place[1] * 4 + place[2]]
-    limits = []
-    for i in range(4):
-        order = order_ref[block_of(place, i, 0)]
-        limit = jnp.where(order < mine, 4096, -4096)
-        limits.append(jnp.where(order == mine, -HALF * place[0], limit))
     ahead_by = lane - lax.broadcasted_iota(jnp.int32, (rows, HALF), 0)
     scores = scores_of(q_ref[0], keys)
     for h in range(4):
         ahead = scores_of(q_ref[h + 1], keys) if h < 3 else None
         parts = [
-            jnp.where(ahead_by <= limit, part, MASKED)
-            for limit, part in zip(limits, pieces_of(scores))
+            jnp.where(ahead_by <= seen_ref[i : i + 1, :], part, MASKED)
+            for i, part in enumerate(pieces_of(scores))
         ]
         floor = jnp.full((rows, HALF), FLOOR, f32)
         weights, peak, total, _ = soften(parts, floor, None)
@@ -146,60 +145,102 @@
         scores = ahead
 
 
-def more_kernel(parts_in, order_ref, place_ref, q_ref, state_ref, *refs):
+def more_kernel(parts_in, seen_ref, q_ref, state_ref, *refs):
     keys = keys_of(refs[:-1])
     out = refs[-1]
     scores = scores_of(q_ref[0], keys)
     for h in range(4):
         ahead = scores_of(q_ref[h + 1], keys) if h < 3 else None
-        parts = masked_pieces(scores, order_ref, place_ref, parts_in)
+        parts = masked_pieces(scores, seen_ref, parts_in)
         weights, peak, total, keep = soften(parts, state_ref[h, :, PEAK], state_ref[h, :, TOTAL])
         numer = scaled(state_ref[h, :, :WIDTH], keep) + mix(weights, keys)
         put_state(out, h, numer, peak, total)
         scores = ahead
 
 
-def last_kernel(parts_in, order_ref, place_ref, q_ref, state_ref, other_ref, kv_ref, out):
+def send_kernel(parts_in, seen_ref, q_ref, state_ref, *refs):
+    keys = keys_of(refs[:-1])
+    out = refs[-1]
+    scores = scores_of(q_ref[0], keys)
+    rows = q_ref.shape[1]
+    lane = lax.broadcasted_iota(jnp.int32, (rows, HALF), 1)
+    for h in range(4):
+        ahead = scores_of(q_ref[h + 1], keys) if h < 3 else None
+        parts = masked_pieces(scores, seen_ref, parts_in)
+        weights, peak, total, keep = soften(parts, state_ref[h, :, PEAK], state_ref[h, :, TOTAL])
+        total = jnp.broadcast_to(jnp.sum(total, axis=1, keepdims=True), (rows, HALF))
+        some = total > 0.0
+        share = jnp.where(some, 1.0 / jnp.where(some, total, 1.0), 0.0)
+        size = jnp.log2(jnp.where(some, total, 1.0)) + peak * LOG_SCALE
+        size = jnp.where(some, size, FLOOR)
+        high = size.astype(jnp.bfloat16).astype(f32)
+        middle = (size - high).astype(jnp.bfloat16).astype(f32)
+        low = size - high - middle
+        tag = jnp.where(lane == 0, high, jnp.where(lane == 1, middle, low))
+        out[h, :, WIDTH:] = jnp.where(lane < 3, tag, 0.0).astype(jnp.bfloat16)
+        numer = scaled(state_ref[h, :, :WIDTH], keep * share)
+        for i, part in enumerate(pieces_of(mix(weights, keys))):
+            span = slice(i * HALF, (i + 1) * HALF)
+            out[h, :, span] = (numer[:, span] + part * share).astype(jnp.bfloat16)
+        scores = ahead
+
+
+def last_kernel(parts_in, seen_ref, q_ref, state_ref, other_ref, kv_ref, out, held):
     keys = keys_of([kv_ref])
     scores = scores_of(q_ref[0], keys)
     for h in range(4):
         ahead = scores_of(q_ref[h + 1], keys) if h < 3 else None
-        parts = masked_pieces(scores, order_ref, place_ref, parts_in)
-        peak, other_peak = state_ref[h, :, PEAK], other_ref[h, :, PEAK]
-        floor = jnp.maximum(peak, other_peak)
+        parts = masked_pieces(scores, seen_ref, parts_in)
+        peak = state_ref[h, :, PEAK]
+        size = jnp.sum(other_ref[h, :, WIDTH:].astype(f32), axis=1, keepdims=True)
+        size = jnp.broadcast_to(size, peak.shape)
+        floor = jnp.maximum(peak, size * (1.0 / LOG_SCALE))
         weights, top, added, _ = soften(parts, floor, None)
         mine = jnp.exp2((peak - top) * LOG_SCALE)
-        theirs = jnp.exp2((other_peak - top) * LOG_SCALE)
-        total = state_ref[h, :, TOTAL] * mine + other_ref[h, :, TOTAL] * theirs + added
-        share = 1.0 / jnp.sum(total, axis=1, keepdims=True)
-        numer = scaled(state_ref[h, :, :WIDTH], mine) + scaled(other_ref[h, :, :WIDTH], theirs)
-        numer = numer + mix(weights, keys)
-        out[:, h, :] = (numer * share).astype(jnp.bfloat16)
+        theirs = jnp.exp2(size - top * LOG_SCALE)
+        total = jnp.sum(state_ref[h, :, TOTAL] * mine + added, axis=1, keepdims=True)
+        share = 1.0 / (jnp.broadcast_to(total, peak.shape) + theirs)
+        numer = scaled(state_ref[h, :, :WIDTH], mine * share)
+        numer = numer + scaled(other_ref[h, :, :WIDTH].astype(f32), theirs * share)
+        held[h] = (numer + scaled(mix(weights, keys), share)).astype(jnp.bfloat16)
         scores = ahead
-
-
-def prepare_kernel(latent_ref, rope_ref, out):
+    out[...] = jnp.swapaxes(held[...], 0, 1)
+
+
+def prepare_kernel(order_ref, place_ref, latent_ref, rope_ref, out, seen_ref):
     for h in range(4):
         out[h, :, :WIDTH] = latent_ref[:, h, :]
         rope = rope_ref[:, h * 64 : h * 64 + 64]
         out[h, :, WIDTH:] = jnp.concatenate([rope, jnp.zeros_like(rope)], axis=1)
 
-
-def prepare(latent, rope):
+    @pl.when(pl.program_id(0) == 0)
+    def _():
+        fill_seen(order_ref, place_ref, seen_ref)
+
+
+def prepare(order, place, latent, rope):
     rows, heads, _ = latent.shape
     return pl.pallas_call(
         prepare_kernel,
         grid=(4,),
-        out_shape=jax.ShapeDtypeStruct((heads, rows, QUERY), jnp.bfloat16),
+        out_shape=[
+            jax.ShapeDtypeStruct((heads, rows, QUERY), jnp.bfloat16),
+            jax.ShapeDtypeStruct((16, HALF), jnp.int32),
+        ],
         in_specs=[
+            SM,
+            SM,
             pl.BlockSpec((rows // 4, heads, WIDTH), lambda i: (i, 0, 0)),
             pl.BlockSpec((rows // 4, heads * 64), lambda i: (i, 0)),
         ],
-        out_specs=pl.BlockSpec((heads, rows // 4, QUERY), lambda i: (0, i, 0)),
+        out_specs=[
+            pl.BlockSpec((heads, rows // 4, QUERY), lambda i: (0, i, 0)),
+            pl.BlockSpec((16, HALF), lambda i: (0, 0)),
+        ],
         compiler_params=pltpu.CompilerParams(vmem_limit_bytes=VMEM_MIB * 2**20),
         cost_estimate=pl.CostEstimate(flops=1 << 30, bytes_accessed=2_000_000, transcendentals=0),
         name="prepare",
-    )(latent, rope)
+    )(order, place, latent, rope)
 
 
 def spread_kernel(place_ref, cache_ref, out):
@@ -224,25 +265,20 @@
     return copies.reshape(4 * rows, HALF)
 
 
-VM = pl.BlockSpec(memory_space=pltpu.VMEM)
-SM = pl.BlockSpec(memory_space=pltpu.SMEM)
-
-
-def call(kernel, out_shape, pieces, where, args, aliases=None):
+def call(kernel, out_shape, pieces, args, aliases=None, scratch=()):
     heads, keys = 4, pieces * HALF
     cost = pl.CostEstimate(
         flops=2 * heads * 256 * keys * (WIDTH * 2 + 64) * 2,
         bytes_accessed=4_000_000,
         transcendentals=heads * 256 * keys,
     )
-    args = [*where, *args]
-    specs = [SM] * len(where) + [VM] * (len(args) - len(where))
     return pl.pallas_call(
         kernel,
         out_shape=out_shape,
-        in_specs=specs,
+        in_specs=[VM] * len(args),
         out_specs=[VM] * len(out_shape) if isinstance(out_shape, list) else VM,
         input_output_aliases=aliases or {},
+        scratch_shapes=scratch,
         compiler_params=pltpu.CompilerParams(vmem_limit_bytes=VMEM_MIB * 2**20),
         cost_estimate=cost,
     )(*args)
@@ -253,9 +289,9 @@
     core = lax.axis_index("co")
     x, y = lax.axis_index("x"), lax.axis_index("yl")
     where = [group_order, jnp.stack([core, x, y]).astype(jnp.int32)]
-    copies = spread(latent_cache, where[1])
+    copies = spread(pltpu.with_memory_space_constraint(latent_cache, pltpu.HBM), where[1])
     bundle = lax.all_to_all(copies, RING, 0, 0, axis_index_groups=near_groups(), tiled=True)
-    queries = prepare(query_latent, query_rope)
+    queries, seen = prepare(*where, query_latent, query_rope)
     bundle = bundle.reshape(4, WIDTH + 64, HALF)
     far = []
     for shift in (1, -1, 2):
@@ -266,19 +302,22 @@
 
     def more(queries, state_in, *parts):
         kernel = functools.partial(more_kernel, parts)
-        args = [queries, state_in, *(far[part] for part in parts)]
-        return call(kernel, state, 4 * len(parts), where, args, {3: 0})
-
-    own = call(near_kernel, state, 4, where, [queries, bundle])
+        args = [seen, queries, state_in, *(far[part] for part in parts)]
+        return call(kernel, state, 4 * len(parts), args, {2: 0})
+
     packed = jax.ShapeDtypeStruct(twin.shape, twin.dtype)
-    sib, twin = call(near_kernel, [state, packed], 4, where, [twin, bundle])
+    own = call(near_kernel, state, 4, [seen, queries, bundle])
+    sib, twin = call(near_kernel, [state, packed], 4, [seen, twin, bundle])
     sib = more(twin, sib, 0)
-    sib = more(twin, sib, 1, 2)
+    own = more(queries, own, 0)
+    send = functools.partial(send_kernel, (1, 2))
+    sib = call(send, packed, 8, [seen, twin, sib, far[1], far[2]])
     other = lax.ppermute(sib, "co", [(0, 1), (1, 0)])
-    own = more(queries, own, 0, 1)
+    own = more(queries, own, 1)
     out = jax.ShapeDtypeStruct((rows, heads, WIDTH), jnp.bfloat16)
     last = functools.partial(last_kernel, (2,))
-    return call(last, out, 4, where, [queries, own, other, far[2]])
+    held = pltpu.VMEM((heads, rows, WIDTH), jnp.bfloat16)
+    return call(last, out, 4, [seen, queries, own, other, far[2]], scratch=[held])
 
 
 def solution(mesh):

time: 66.1 us -> 66 us (level)
  Pallas kernels: 23.4 us -> 21.5 us
  waiting for transfers between devices: 6.2 us -> 7.37 us
    pallas_call x7 -> x8, Pallas kernels: 22.7 us -> 19.9 us  [the longest x7 17 us: call(): pl.pallas_call(kernel, out_shape=out_shape, in_specs=[VM] * len(args), ou...]
    ppermute x3, waiting for transfers between devices: 6.2 us -> 7.36 us  [split_permute(): return lax.ppermute(value, RING, pairs)]
    pallas_call x1, Pallas kernels: 0.65 us -> 1.53 us  [spread(): pl.pallas_call(spread_kernel, grid_spec=pltpu.PrefetchScalarGridSpec(num_...]
    unnamed x8 -> x6, local copies, waits for them, and re-layouts: 2.18 us -> 2.78 us
  transfers between devices with their start and end apart: 5 -> 5, of which waited for: 2 -> 2; matrix products, arithmetic and copies ran while one was open for 0% -> 0% of each run, Pallas kernels for 19% -> 17%
where the time goes in v1:
time: 66 us; the launch traced here: 65.6 us
  starting transfers between devices  23.9 us (36%)
  Pallas kernels  21.5 us (33%)
  blocking collectives  9.81 us (15%)
  waiting for transfers between devices  7.37 us (11%)
  local copies, waits for them, and re-layouts  2.78 us (4%)
    pallas_call x7, Pallas kernels, call(): pl.pallas_call(kernel, out_shape=out_shape, in_specs=[VM] * len(args), ou...  17 us
    all_to_all x1, blocking collectives, attend(): lax.all_to_all(copies, RING, 0, 0, axis_index_groups=near_groups(), tiled...  9.81 us
    ppermute x1, starting transfers between devices, attend(): twin = lax.ppermute(queries, 'co', [(0, 1), (1, 0)])  8.75 us
    ppermute x3, starting transfers between devices, split_permute(): return lax.ppermute(value, RING, pairs)  8.4 us
    ppermute x3, waiting for transfers between devices, split_permute(): return lax.ppermute(value, RING, pairs)  7.36 us
    ppermute x1, starting transfers between devices, attend(): other = lax.ppermute(sib, 'co', [(0, 1), (1, 0)])  6.8 us
    pallas_call x1, Pallas kernels, prepare(): pl.pallas_call(prepare_kernel, grid=(4,), out_shape=[jax.ShapeDtypeStruct...  2.99 us
    unnamed x6, local copies, waits for them, and re-layouts  2.78 us
  transfers between devices with their start and end apart: 5, of which 2 were waited for; matrix products, arithmetic and copies ran while one was open for 0% of the time, Pallas kernels for 17%

profile of v1, /device:TPU:1, one launch (start us, length us, event | category | flops | bytes accessed | tf_op | source)
XLA Modules:
  0.0 65.6 jit_solution(6876010722360585751)
XLA Ops:
  0.0 0.1 pad_add_fusion.place_ref
  0.1 0.0 copy-start
  0.1 1.2 %copy-done = bf16[256,4,512]{2,1,0:T(4,128)(2,1)S(1)} copy-done((bf16[256,4,512]{2,1,0:T(4,128)(2,1)S(1)}, bf16[256,4,512]{2,1,0:T(4,128)(2,1)}, u32[]{:S(2)}) %copy-start) | copy-done | bytes 1048600
  1.3 0.0 copy-start.1
  1.3 0.9 %copy-done.1 = bf16[256,256]{1,0:T(8,128)(2,1)S(1)} copy-done((bf16[256,256]{1,0:T(8,128)(2,1)S(1)}, bf16[256,256]{1,0:T(8,128)(2,1)}, u32[]{:S(2)}) %copy-start.1) | copy-done | bytes 131096
  2.2 0.0 copy-start.2
  2.2 0.7 copy-done.2
  2.9 3.0 %prepare.1 = (bf16[4,256,640]{2,1,0:T(8,128)(2,1)S(1)}, s32[16,128]{1,0:T(8,128)S(1)}) custom-call(s32[16]{0:T(128)S(1)} %copy-done.2, s32[3]{0:T(128)S(1)} %pad_add_fusion.place_ref, bf16[256,4,512]{2,1,0:T(4,128)(2,1)S(1)} %copy-done, bf16[256,256]{1,0:T(8,128)(2,1)S(1)} %copy-done.1), custom_call_target="tpu_custom_call" | custom-call | flops 1073741824 | bytes 2000000 | tf_op jit(solution)/shard_map/prepare/pallas_call | solution.py:223
  5.9 8.7 %collective-permute-start.2 = (bf16[4,256,640]{2,1,0:T(8,128)(2,1)S(1)}, bf16[4,256,640]{2,1,0:T(8,128)(2,1)S(1)}, u32[]{:S(2)}, u32[]{:S(2)}) collective-permute-start(bf16[4,256,640]{2,1,0:T(8,128)(2,1)S(1)} %get-tuple-element.10.q_ref), channel_id=1, source_target_pairs={{0,16},{16,0},{1,17},{17,1},{2,18},{18,2},{3,19},{19,3},{4,20},{20... | collective-permute-start | bytes 3932168 | tf_op jit(solution)/shard_map/ppermute | solution.py:299
  14.6 1.5 %spread.1 = bf16[4,576,128]{2,1,0:T(8,128)(2,1)S(1)} custom-call(s32[3]{0:T(128)S(1)} %pad_add_fusion.place_ref, bf16[576,256]{1,0:T(8,128)(2,1)} %cache_ref.1), custom_call_target="tpu_custom_call" | custom-call | tf_op jit(solution)/shard_map/spread/pallas_call | solution.py:253
  16.1 9.8 %all_to_all.6.kv_ref = bf16[4,576,128]{2,1,0:T(8,128)(2,1)S(1)} all-to-all(bf16[4,576,128]{2,1,0:T(8,128)(2,1)S(1)} %spread.1), channel_id=1, replica_groups={{0,1,2,3},{4,5,6,7},{8,9,10,11},{12,13,14,15},{16,20,24,28},{17,21,25,2..., dimensions={0} | all-to-all | bytes 1179648 | tf_op jit(solution)/shard_map/all_to_all | solution.py:293
  26.0 1.9 %collective-permute-start = (bf16[4,576,128]{2,1,0:T(8,128)(2,1)S(1)}, bf16[4,576,128]{2,1,0:T(8,128)(2,1)S(1)}, u32[]{:S(2)}, u32[]{:S(2)}) collective-permute-start(bf16[4,576,128]{2,1,0:T(8,128)(2,1)S(1)} %all_to_all.6.kv_ref), channel_id=1, source_target_pairs={{0,4},{4,8},{8,12},{12,0},{16,17},{20,21},{24,25},{28,29},{1,5},{5... | collective-permute-start | bytes 1769480 | tf_op jit(solution)/shard_map/ppermute | solution.py:46
  27.9 4.6 %collective-permute-start.1 = (bf16[4,576,128]{2,1,0:T(8,128)(2,1)S(1)}, bf16[4,576,128]{2,1,0:T(8,128)(2,1)S(1)}, u32[]{:S(2)}, u32[]{:S(2)}) collective-permute-start(bf16[4,576,128]{2,1,0:T(8,128)(2,1)S(1)} %all_to_all.6.kv_ref), channel_id=1, source_target_pairs={{0,12},{4,0},{8,4},{12,8},{16,51},{20,55},{24,59},{28,63},{1,13},{... | collective-permute-start | bytes 1769480 | tf_op jit(solution)/shard_map/ppermute | solution.py:46
  32.5 1.9 %collective-permute-start.3 = (bf16[4,576,128]{2,1,0:T(8,128)(2,1)S(1)}, bf16[4,576,128]{2,1,0:T(8,128)(2,1)S(1)}, u32[]{:S(2)}, u32[]{:S(2)}) collective-permute-start(bf16[4,576,128]{2,1,0:T(8,128)(2,1)S(1)} %all_to_all.6.kv_ref), channel_id=1, source_target_pairs={{0,8},{4,12},{8,0},{12,4},{16,18},{20,22},{24,26},{28,30},{1,9},{5... | collective-permute-start | bytes 1769480 | tf_op jit(solution)/shard_map/ppermute | solution.py:46
  34.4 0.0 collective-permute-done.2.q_ref
  34.4 1.7 %shard_map.49 = (f32[4,256,768]{2,1,0:T(8,128)S(1)}, bf16[4,256,640]{2,1,0:T(8,128)(2,1)S(1)}) custom-call(s32[16,128]{1,0:T(8,128)S(1)} %get-tuple-element.9.seen_ref, bf16[4,256,640]{2,1,0:T(8,128)(2,1)S(1)} %collective-permute-done.2.q_ref, bf16[4,576,128]{2,1,0:T(8,128)(2,1)S(1)} %all_to_all.6.kv_ref), custom_call_target="tpu_custom_call" | custom-call | flops 2281701376 | bytes 4000000 | tf_op jit(solution)/shard_map/pallas_call | solution.py:275
  36.1 2.0 %collective-permute-done.refs_0_ = bf16[4,576,128]{2,1,0:T(8,128)(2,1)S(1)} collective-permute-done((bf16[4,576,128]{2,1,0:T(8,128)(2,1)S(1)}, bf16[4,576,128]{2,1,0:T(8,128)(2,1)S(1)}, u32[]{:S(2)}, u32[]{:S(2)}) %collective-permute-start) | collective-permute-done | bytes 589856 | tf_op jit(solution)/shard_map/ppermute | solution.py:46
  38.1 2.1 %shard_map.50.state_ref = f32[4,256,768]{2,1,0:T(8,128)S(1)} custom-call(s32[16,128]{1,0:T(8,128)S(1)} %get-tuple-element.9.seen_ref, bf16[4,256,640]{2,1,0:T(8,128)(2,1)S(1)} %get-tuple-element.11.q_ref, f32[4,256,768]{2,1,0:T(8,128)S(1)} %get-tuple-element.12.state_ref, ...), custom_call_target="tpu_custom_call", output_to_operand_aliasing={{}: (2, {})} | custom-call | flops 2281701376 | bytes 4000000 | tf_op jit(solution)/shard_map/pallas_call | solution.py:275
  40.2 5.4 %collective-permute-done.1.refs_0_ = bf16[4,576,128]{2,1,0:T(8,128)(2,1)S(1)} collective-permute-done((bf16[4,576,128]{2,1,0:T(8,128)(2,1)S(1)}, bf16[4,576,128]{2,1,0:T(8,128)(2,1)S(1)}, u32[]{:S(2)}, u32[]{:S(2)}) %collective-permute-start.1) | collective-permute-done | bytes 589856 | tf_op jit(solution)/shard_map/ppermute | solution.py:46
  45.6 0.0 collective-permute-done.3.refs_1_.kv_ref
  45.6 3.8 %shard_map.51 = bf16[4,256,640]{2,1,0:T(8,128)(2,1)S(1)} custom-call(s32[16,128]{1,0:T(8,128)S(1)} %get-tuple-element.9.seen_ref, bf16[4,256,640]{2,1,0:T(8,128)(2,1)S(1)} %get-tuple-element.11.q_ref, f32[4,256,768]{2,1,0:T(8,128)S(1)} %shard_map.50.state_ref, bf16[4,576,128]{2,1,0:T(8,128)(2,1)S(1)} %collective-permute-done.1.refs_0_, ...), custom_call_target="tpu_custom_call" | custom-call | flops 4563402752 | bytes 4000000 | tf_op jit(solution)/shard_map/pallas_call | solution.py:275
  49.4 6.8 %collective-permute-start.4 = (bf16[4,256,640]{2,1,0:T(8,128)(2,1)S(1)}, bf16[4,256,640]{2,1,0:T(8,128)(2,1)S(1)}, u32[]{:S(2)}, u32[]{:S(2)}) collective-permute-start(bf16[4,256,640]{2,1,0:T(8,128)(2,1)S(1)} %shard_map.51), channel_id=1, source_target_pairs={{0,16},{16,0},{1,17},{17,1},{2,18},{18,2},{3,19},{19,3},{4,20},{20... | collective-permute-start | bytes 3932168 | tf_op jit(solution)/shard_map/ppermute | solution.py:315
  56.2 1.6 %shard_map.46.state_ref = f32[4,256,768]{2,1,0:T(8,128)S(1)} custom-call(s32[16,128]{1,0:T(8,128)S(1)} %get-tuple-element.9.seen_ref, bf16[4,256,640]{2,1,0:T(8,128)(2,1)S(1)} %get-tuple-element.10.q_ref, bf16[4,576,128]{2,1,0:T(8,128)(2,1)S(1)} %all_to_all.6.kv_ref), custom_call_target="tpu_custom_call" | custom-call | flops 2281701376 | bytes 4000000 | tf_op jit(solution)/shard_map/pallas_call | solution.py:275
  57.8 2.1 %shard_map.47.state_ref = f32[4,256,768]{2,1,0:T(8,128)S(1)} custom-call(s32[16,128]{1,0:T(8,128)S(1)} %get-tuple-element.9.seen_ref, bf16[4,256,640]{2,1,0:T(8,128)(2,1)S(1)} %get-tuple-element.10.q_ref, f32[4,256,768]{2,1,0:T(8,128)S(1)} %shard_map.46.state_ref, bf16[4,576,128]{2,1,0:T(8,128)(2,1)S(1)} %collective-permute-done.refs_0_), custom_call_target="tpu_custom_call", output_to_operand_aliasing={{}: (2, {})} | custom-call | flops 2281701376 | bytes 4000000 | tf_op jit(solution)/shard_map/pallas_call | solution.py:275
  59.9 2.1 %shard_map.48.state_ref = f32[4,256,768]{2,1,0:T(8,128)S(1)} custom-call(s32[16,128]{1,0:T(8,128)S(1)} %get-tuple-element.9.seen_ref, bf16[4,256,640]{2,1,0:T(8,128)(2,1)S(1)} %get-tuple-element.10.q_ref, f32[4,256,768]{2,1,0:T(8,128)S(1)} %shard_map.47.state_ref, bf16[4,576,128]{2,1,0:T(8,128)(2,1)S(1)} %collective-permute-done.1.refs_0_), custom_call_target="tpu_custom_call", output_to_operand_aliasing={{}: (2, {})} | custom-call | flops 2281701376 | bytes 4000000 | tf_op jit(solution)/shard_map/pallas_call | solution.py:275
  62.1 0.0 collective-permute-done.4.other_ref
  62.1 3.5 %shard_map.52 = bf16[256,4,512]{2,1,0:T(4,128)(2,1)} custom-call(s32[16,128]{1,0:T(8,128)S(1)} %get-tuple-element.9.seen_ref, bf16[4,256,640]{2,1,0:T(8,128)(2,1)S(1)} %get-tuple-element.10.q_ref, f32[4,256,768]{2,1,0:T(8,128)S(1)} %shard_map.48.state_ref, bf16[4,256,640]{2,1,0:T(8,128)(2,1)S(1)} %collective-permute-done.4.other_ref, ...), custom_call_target="tpu_custom_call" | custom-call | flops 2281701376 | bytes 4000000 | tf_op jit(solution)/shard_map/pallas_call | solution.py:275
Async XLA Ops:
  0.1 1.2 %copy-start = (bf16[256,4,512]{2,1,0:T(4,128)(2,1)S(1)}, bf16[256,4,512]{2,1,0:T(4,128)(2,1)}, u32[]{:S(2)}) copy-start(bf16[256,4,512]{2,1,0:T(4,128)(2,1)} %latent_ref.1) | copy-start | bytes 3145732
  1.3 0.9 %copy-start.1 = (bf16[256,256]{1,0:T(8,128)(2,1)S(1)}, bf16[256,256]{1,0:T(8,128)(2,1)}, u32[]{:S(2)}) copy-start(bf16[256,256]{1,0:T(8,128)(2,1)} %rope_ref.1) | copy-start | bytes 393220
  2.2 0.7 copy-start.2
  5.9 28.5 %collective-permute-start.2 = (bf16[4,256,640]{2,1,0:T(8,128)(2,1)S(1)}, bf16[4,256,640]{2,1,0:T(8,128)(2,1)S(1)}, u32[]{:S(2)}, u32[]{:S(2)}) collective-permute-start(bf16[4,256,640]{2,1,0:T(8,128)(2,1)S(1)} %get-tuple-element.10.q_ref), channel_id=1, source_target_pairs={{0,16},{16,0},{1,17},{17,1},{2,18},{18,2},{3,19},{19,3},{4,20},{20... | collective-permute-start | bytes 3932168 | tf_op jit(solution)/shard_map/ppermute | solution.py:299
  26.0 12.1 %collective-permute-start = (bf16[4,576,128]{2,1,0:T(8,128)(2,1)S(1)}, bf16[4,576,128]{2,1,0:T(8,128)(2,1)S(1)}, u32[]{:S(2)}, u32[]{:S(2)}) collective-permute-start(bf16[4,576,128]{2,1,0:T(8,128)(2,1)S(1)} %all_to_all.6.kv_ref), channel_id=1, source_target_pairs={{0,4},{4,8},{8,12},{12,0},{16,17},{20,21},{24,25},{28,29},{1,5},{5... | collective-permute-start | bytes 1769480 | tf_op jit(solution)/shard_map/ppermute | solution.py:46
  27.9 17.7 %collective-permute-start.1 = (bf16[4,576,128]{2,1,0:T(8,128)(2,1)S(1)}, bf16[4,576,128]{2,1,0:T(8,128)(2,1)S(1)}, u32[]{:S(2)}, u32[]{:S(2)}) collective-permute-start(bf16[4,576,128]{2,1,0:T(8,128)(2,1)S(1)} %all_to_all.6.kv_ref), channel_id=1, source_target_pairs={{0,12},{4,0},{8,4},{12,8},{16,51},{20,55},{24,59},{28,63},{1,13},{... | collective-permute-start | bytes 1769480 | tf_op jit(solution)/shard_map/ppermute | solution.py:46
  32.5 13.1 %collective-permute-start.3 = (bf16[4,576,128]{2,1,0:T(8,128)(2,1)S(1)}, bf16[4,576,128]{2,1,0:T(8,128)(2,1)S(1)}, u32[]{:S(2)}, u32[]{:S(2)}) collective-permute-start(bf16[4,576,128]{2,1,0:T(8,128)(2,1)S(1)} %all_to_all.6.kv_ref), channel_id=1, source_target_pairs={{0,8},{4,12},{8,0},{12,4},{16,18},{20,22},{24,26},{28,30},{1,9},{5... | collective-permute-start | bytes 1769480 | tf_op jit(solution)/shard_map/ppermute | solution.py:46
  49.4 12.7 %collective-permute-start.4 = (bf16[4,256,640]{2,1,0:T(8,128)(2,1)S(1)}, bf16[4,256,640]{2,1,0:T(8,128)(2,1)S(1)}, u32[]{:S(2)}, u32[]{:S(2)}) collective-permute-start(bf16[4,256,640]{2,1,0:T(8,128)(2,1)S(1)} %shard_map.51), channel_id=1, source_target_pairs={{0,16},{16,0},{1,17},{17,1},{2,18},{18,2},{3,19},{19,3},{4,20},{20... | collective-permute-start | bytes 3932168 | tf_op jit(solution)/shard_map/ppermute | solution.py:315

commit v2 on v1

--- a/solution.py
+++ b/solution.py
@@ -125,35 +125,41 @@
     ref[h, :, TOTAL] = total
 
 
-def near_kernel(seen_ref, q_ref, kv_ref, out, *keep):
-    for ref in keep:
-        ref[...] = q_ref[...]
+def near_kernel(seen_ref, own_ref, twin_ref, kv_ref, own_out, sib_out, keep_ref):
     keys = keys_of([kv_ref])
-    rows = q_ref.shape[1]
+    rows = own_ref.shape[1]
     lane = lax.broadcasted_iota(jnp.int32, (rows, HALF), 1)
     ahead_by = lane - lax.broadcasted_iota(jnp.int32, (rows, HALF), 0)
-    scores = scores_of(q_ref[0], keys)
-    for h in range(4):
-        ahead = scores_of(q_ref[h + 1], keys) if h < 3 else None
+    work = [(own_ref, own_out, h) for h in range(4)] + [(twin_ref, sib_out, h) for h in range(4)]
+    scores = scores_of(own_ref[0], keys)
+    for i, (_, out, h) in enumerate(work):
+        ahead = None
+        if i + 1 < len(work):
+            ahead = scores_of(work[i + 1][0][work[i + 1][2]], keys)
         parts = [
-            jnp.where(ahead_by <= seen_ref[i : i + 1, :], part, MASKED)
-            for i, part in enumerate(pieces_of(scores))
+            jnp.where(ahead_by <= seen_ref[j : j + 1, :], part, MASKED)
+            for j, part in enumerate(pieces_of(scores))
         ]
         floor = jnp.full((rows, HALF), FLOOR, f32)
         weights, peak, total, _ = soften(parts, floor, None)
         put_state(out, h, mix(weights, keys), peak, total)
         scores = ahead
-
-
-def more_kernel(parts_in, seen_ref, q_ref, state_ref, *refs):
-    keys = keys_of(refs[:-1])
-    out = refs[-1]
-    scores = scores_of(q_ref[0], keys)
-    for h in range(4):
-        ahead = scores_of(q_ref[h + 1], keys) if h < 3 else None
+    keep_ref[...] = twin_ref[...]
+
+
+def more_kernel(parts_in, count, seen_ref, *refs):
+    queries, states = refs[:count], refs[count : 2 * count]
+    outs = refs[len(refs) - count :]
+    keys = keys_of(refs[2 * count : len(refs) - count])
+    work = [(q, s, out, h) for q, s, out in zip(queries, states, outs) for h in range(4)]
+    scores = scores_of(work[0][0][0], keys)
+    for i, (_, state, out, h) in enumerate(work):
+        ahead = None
+        if i + 1 < len(work):
+            ahead = scores_of(work[i + 1][0][work[i + 1][3]], keys)
         parts = masked_pieces(scores, seen_ref, parts_in)
-        weights, peak, total, keep = soften(parts, state_ref[h, :, PEAK], state_ref[h, :, TOTAL])
-        numer = scaled(state_ref[h, :, :WIDTH], keep) + mix(weights, keys)
+        weights, peak, total, keep = soften(parts, state[h, :, PEAK], state[h, :, TOTAL])
+        numer = scaled(state[h, :, :WIDTH], keep) + mix(weights, keys)
         put_state(out, h, numer, peak, total)
         scores = ahead
 
@@ -185,26 +191,36 @@
         scores = ahead
 
 
-def last_kernel(parts_in, seen_ref, q_ref, state_ref, other_ref, kv_ref, out, held):
+def last_kernel(parts_in, seen_ref, q_ref, state_ref, other_ref, kv_ref, out, held, sems):
     keys = keys_of([kv_ref])
-    scores = scores_of(q_ref[0], keys)
-    for h in range(4):
-        ahead = scores_of(q_ref[h + 1], keys) if h < 3 else None
+    heads, rows, _ = q_ref.shape
+    step = rows // 4
+    span = lambda c: slice(c * step, (c + 1) * step)
+    flat = lambda value: value.reshape(heads * step, value.shape[-1])
+    scores = scores_of(flat(q_ref[:, span(0), :]), keys)
+    copies = []
+    for c in range(4):
+        ahead = scores_of(flat(q_ref[:, span(c + 1), :]), keys) if c < 3 else None
         parts = masked_pieces(scores, seen_ref, parts_in)
-        peak = state_ref[h, :, PEAK]
-        size = jnp.sum(other_ref[h, :, WIDTH:].astype(f32), axis=1, keepdims=True)
-        size = jnp.broadcast_to(size, peak.shape)
+        peak = flat(state_ref[:, span(c), PEAK])
+        size = flat(other_ref[:, span(c), WIDTH:]).astype(f32)
+        size = jnp.broadcast_to(jnp.sum(size, axis=1, keepdims=True), peak.shape)
         floor = jnp.maximum(peak, size * (1.0 / LOG_SCALE))
         weights, top, added, _ = soften(parts, floor, None)
         mine = jnp.exp2((peak - top) * LOG_SCALE)
         theirs = jnp.exp2(size - top * LOG_SCALE)
-        total = jnp.sum(state_ref[h, :, TOTAL] * mine + added, axis=1, keepdims=True)
+        total = flat(state_ref[:, span(c), TOTAL]) * mine + added
+        total = jnp.sum(total, axis=1, keepdims=True)
         share = 1.0 / (jnp.broadcast_to(total, peak.shape) + theirs)
-        numer = scaled(state_ref[h, :, :WIDTH], mine * share)
-        numer = numer + scaled(other_ref[h, :, :WIDTH].astype(f32), theirs * share)
-        held[h] = (numer + scaled(mix(weights, keys), share)).astype(jnp.bfloat16)
+        numer = scaled(flat(state_ref[:, span(c), :WIDTH]), mine * share)
+        numer = numer + scaled(flat(other_ref[:, span(c), :WIDTH]).astype(f32), theirs * share)
+        numer = (numer + scaled(mix(weights, keys), share)).astype(jnp.bfloat16)
+        held[span(c)] = jnp.swapaxes(numer.reshape(heads, step, WIDTH), 0, 1)
+        copies.append(pltpu.make_async_copy(held.at[span(c)], out.at[span(c)], sems.at[c]))
+        copies[-1].start()
         scores = ahead
-    out[...] = jnp.swapaxes(held[...], 0, 1)
+    for copy in copies:
+        copy.wait()
 
 
 def prepare_kernel(order_ref, place_ref, latent_ref, rope_ref, out, seen_ref):
@@ -265,7 +281,7 @@
     return copies.reshape(4 * rows, HALF)
 
 
-def call(kernel, out_shape, pieces, args, aliases=None, scratch=()):
+def call(kernel, out_shape, pieces, args, aliases=None, scratch=(), out_spec=VM):
     heads, keys = 4, pieces * HALF
     cost = pl.CostEstimate(
         flops=2 * heads * 256 * keys * (WIDTH * 2 + 64) * 2,
@@ -276,7 +292,7 @@
         kernel,
         out_shape=out_shape,
         in_specs=[VM] * len(args),
-        out_specs=[VM] * len(out_shape) if isinstance(out_shape, list) else VM,
+        out_specs=[VM] * len(out_shape) if isinstance(out_shape, list) else out_spec,
         input_output_aliases=aliases or {},
         scratch_shapes=scratch,
         compiler_params=pltpu.CompilerParams(vmem_limit_bytes=VMEM_MIB * 2**20),
@@ -300,24 +316,28 @@
 
     state = jax.ShapeDtypeStruct((heads, rows, STATE), f32)
 
-    def more(queries, state_in, *parts):
-        kernel = functools.partial(more_kernel, parts)
-        args = [seen, queries, state_in, *(far[part] for part in parts)]
-        return call(kernel, state, 4 * len(parts), args, {2: 0})
+    def more(queries, states, *parts):
+        count = len(queries)
+        kernel = functools.partial(more_kernel, parts, count)
+        args = [seen, *queries, *states, *(far[part] for part in parts)]
+        aliases = {1 + count + i: i for i in range(count)}
+        return call(kernel, [state] * count, 4 * len(parts) * count, args, aliases)
 
     packed = jax.ShapeDtypeStruct(twin.shape, twin.dtype)
-    own = call(near_kernel, state, 4, [seen, queries, bundle])
-    sib, twin = call(near_kernel, [state, packed], 4, [seen, twin, bundle])
-    sib = more(twin, sib, 0)
-    own = more(queries, own, 0)
-    send = functools.partial(send_kernel, (1, 2))
-    sib = call(send, packed, 8, [seen, twin, sib, far[1], far[2]])
+    args = [seen, queries, twin, bundle]
+    own, sib, twin = call(near_kernel, [state, state, packed], 8, args)
+    own, sib = more([queries, twin], [own, sib], 2)
+    (sib,) = more([twin], [sib], 0)
+    send = functools.partial(send_kernel, (1,))
+    sib = call(send, packed, 4, [seen, twin, sib, far[1]])
     other = lax.ppermute(sib, "co", [(0, 1), (1, 0)])
-    own = more(queries, own, 1)
+    (own,) = more([queries], [own], 0)
     out = jax.ShapeDtypeStruct((rows, heads, WIDTH), jnp.bfloat16)
-    last = functools.partial(last_kernel, (2,))
-    held = pltpu.VMEM((heads, rows, WIDTH), jnp.bfloat16)
-    return call(last, out, 4, [seen, queries, own, other, far[2]], scratch=[held])
+    last = functools.partial(last_kernel, (1,))
+    scratch = [pltpu.VMEM((rows, heads, WIDTH), jnp.bfloat16), pltpu.SemaphoreType.DMA((4,))]
+    args = [seen, queries, own, other, far[1]]
+    hbm = pl.BlockSpec(memory_space=pltpu.HBM)
+    return call(last, out, 4, args, scratch=scratch, out_spec=hbm)
 
 
 def solution(mesh):

time: 66 us -> 68 us (1.030)
  starting transfers between devices: 23.9 us -> 29.4 us
  waiting for transfers between devices: 7.37 us -> 4.07 us
    ppermute x1, starting transfers between devices: 6.8 us -> 12.3 us  [attend(): other = lax.ppermute(sib, 'co', [(0, 1), (1, 0)])]
    ppermute x3, waiting for transfers between devices: 7.36 us -> 3.74 us  [split_permute(): return lax.ppermute(value, RING, pairs)]
    pallas_call x7 -> x6, Pallas kernels: 17 us -> 16.7 us  [call(): pl.pallas_call(kernel, out_shape=out_shape, in_specs=[VM] * len(args), ou...]
  transfers between devices with their start and end apart: 5 -> 5, of which waited for: 2 -> 3; matrix products, arithmetic and copies ran while one was open for 0% -> 0% of each run, Pallas kernels for 17% -> 19%
where the time goes in v2:
time: 68 us; the launch traced here: 67.7 us
  starting transfers between devices  29.4 us (43%)
  Pallas kernels  21.3 us (31%)
  blocking collectives  9.81 us (14%)
  waiting for transfers between devices  4.07 us (6%)
  local copies, waits for them, and re-layouts  2.78 us (4%)
    pallas_call x6, Pallas kernels, call(): pl.pallas_call(kernel, out_shape=out_shape, in_specs=[VM] * len(args), ou...  16.7 us
    ppermute x1, starting transfers between devices, attend(): other = lax.ppermute(sib, 'co', [(0, 1), (1, 0)])  12.3 us
    all_to_all x1, blocking collectives, attend(): lax.all_to_all(copies, RING, 0, 0, axis_index_groups=near_groups(), tiled...  9.81 us
    ppermute x1, starting transfers between devices, attend(): twin = lax.ppermute(queries, 'co', [(0, 1), (1, 0)])  8.75 us
    ppermute x3, starting transfers between devices, split_permute(): return lax.ppermute(value, RING, pairs)  8.4 us
    ppermute x3, waiting for transfers between devices, split_permute(): return lax.ppermute(value, RING, pairs)  3.74 us
    pallas_call x1, Pallas kernels, prepare(): pl.pallas_call(prepare_kernel, grid=(4,), out_shape=[jax.ShapeDtypeStruct...  2.99 us
    unnamed x6, local copies, waits for them, and re-layouts  2.78 us
  transfers between devices with their start and end apart: 5, of which 3 were waited for; matrix products, arithmetic and copies ran while one was open for 0% of the time, Pallas kernels for 19%

profile of v2, /device:TPU:1, one launch (start us, length us, event | category | flops | bytes accessed | tf_op | source)
XLA Modules:
  0.0 67.7 jit_solution(12245263417119682003)
XLA Ops:
  0.0 0.1 pad_add_fusion.place_ref
  0.1 0.0 copy-start
  0.1 1.2 %copy-done = bf16[256,4,512]{2,1,0:T(4,128)(2,1)S(1)} copy-done((bf16[256,4,512]{2,1,0:T(4,128)(2,1)S(1)}, bf16[256,4,512]{2,1,0:T(4,128)(2,1)}, u32[]{:S(2)}) %copy-start) | copy-done | bytes 1048600
  1.3 0.0 copy-start.1
  1.3 0.9 %copy-done.1 = bf16[256,256]{1,0:T(8,128)(2,1)S(1)} copy-done((bf16[256,256]{1,0:T(8,128)(2,1)S(1)}, bf16[256,256]{1,0:T(8,128)(2,1)}, u32[]{:S(2)}) %copy-start.1) | copy-done | bytes 131096
  2.2 0.0 copy-start.2
  2.2 0.7 copy-done.2
  2.9 3.0 %prepare.1 = (bf16[4,256,640]{2,1,0:T(8,128)(2,1)S(1)}, s32[16,128]{1,0:T(8,128)S(1)}) custom-call(s32[16]{0:T(128)S(1)} %copy-done.2, s32[3]{0:T(128)S(1)} %pad_add_fusion.place_ref, bf16[256,4,512]{2,1,0:T(4,128)(2,1)S(1)} %copy-done, bf16[256,256]{1,0:T(8,128)(2,1)S(1)} %copy-done.1), custom_call_target="tpu_custom_call" | custom-call | flops 1073741824 | bytes 2000000 | tf_op jit(solution)/shard_map/prepare/pallas_call | solution.py:239
  5.9 8.7 %collective-permute-start = (bf16[4,256,640]{2,1,0:T(8,128)(2,1)S(1)}, bf16[4,256,640]{2,1,0:T(8,128)(2,1)S(1)}, u32[]{:S(2)}, u32[]{:S(2)}) collective-permute-start(bf16[4,256,640]{2,1,0:T(8,128)(2,1)S(1)} %get-tuple-element.13.own_ref.refs_0_.q_ref), channel_id=1, source_target_pairs={{0,16},{16,0},{1,17},{17,1},{2,18},{18,2},{3,19},{19,3},{4,20},{20... | collective-permute-start | bytes 3932168 | tf_op jit(solution)/shard_map/ppermute | solution.py:315
  14.6 1.5 %spread.1 = bf16[4,576,128]{2,1,0:T(8,128)(2,1)S(1)} custom-call(s32[3]{0:T(128)S(1)} %pad_add_fusion.place_ref, bf16[576,256]{1,0:T(8,128)(2,1)} %cache_ref.1), custom_call_target="tpu_custom_call" | custom-call | tf_op jit(solution)/shard_map/spread/pallas_call | solution.py:269
  16.1 9.8 %all_to_all.6.kv_ref = bf16[4,576,128]{2,1,0:T(8,128)(2,1)S(1)} all-to-all(bf16[4,576,128]{2,1,0:T(8,128)(2,1)S(1)} %spread.1), channel_id=1, replica_groups={{0,1,2,3},{4,5,6,7},{8,9,10,11},{12,13,14,15},{16,20,24,28},{17,21,25,2..., dimensions={0} | all-to-all | bytes 1179648 | tf_op jit(solution)/shard_map/all_to_all | solution.py:309
  26.0 1.9 %collective-permute-start.1 = (bf16[4,576,128]{2,1,0:T(8,128)(2,1)S(1)}, bf16[4,576,128]{2,1,0:T(8,128)(2,1)S(1)}, u32[]{:S(2)}, u32[]{:S(2)}) collective-permute-start(bf16[4,576,128]{2,1,0:T(8,128)(2,1)S(1)} %all_to_all.6.kv_ref), channel_id=1, source_target_pairs={{0,8},{4,12},{8,0},{12,4},{16,18},{20,22},{24,26},{28,30},{1,9},{5... | collective-permute-start | bytes 1769480 | tf_op jit(solution)/shard_map/ppermute | solution.py:46
  27.9 2.4 %collective-permute-start.2 = (bf16[4,576,128]{2,1,0:T(8,128)(2,1)S(1)}, bf16[4,576,128]{2,1,0:T(8,128)(2,1)S(1)}, u32[]{:S(2)}, u32[]{:S(2)}) collective-permute-start(bf16[4,576,128]{2,1,0:T(8,128)(2,1)S(1)} %all_to_all.6.kv_ref), channel_id=1, source_target_pairs={{0,4},{4,8},{8,12},{12,0},{16,17},{20,21},{24,25},{28,29},{1,5},{5... | collective-permute-start | bytes 1769480 | tf_op jit(solution)/shard_map/ppermute | solution.py:46
  30.2 4.1 %collective-permute-start.3 = (bf16[4,576,128]{2,1,0:T(8,128)(2,1)S(1)}, bf16[4,576,128]{2,1,0:T(8,128)(2,1)S(1)}, u32[]{:S(2)}, u32[]{:S(2)}) collective-permute-start(bf16[4,576,128]{2,1,0:T(8,128)(2,1)S(1)} %all_to_all.6.kv_ref), channel_id=1, source_target_pairs={{0,12},{4,0},{8,4},{12,8},{16,51},{20,55},{24,59},{28,63},{1,13},{... | collective-permute-start | bytes 1769480 | tf_op jit(solution)/shard_map/ppermute | solution.py:46
  34.4 0.0 collective-permute-done.twin_ref
  34.4 3.1 %shard_map.46 = (f32[4,256,768]{2,1,0:T(8,128)S(1)}, f32[4,256,768]{2,1,0:T(8,128)S(1)}, bf16[4,256,640]{2,1,0:T(8,128)(2,1)S(1)}) custom-call(s32[16,128]{1,0:T(8,128)S(1)} %get-tuple-element.12.seen_ref, bf16[4,256,640]{2,1,0:T(8,128)(2,1)S(1)} %get-tuple-element.13.own_ref.refs_0_.q_ref, bf16[4,256,640]{2,1,0:T(8,128)(2,1)S(1)} %collective-permute-done.twin_ref, ...), custom_call_target="tpu_custom_call" | custom-call | flops 4563402752 | bytes 4000000 | tf_op jit(solution)/shard_map/pallas_call | solution.py:291
  37.5 1.3 %collective-permute-done.1.refs_4_ = bf16[4,576,128]{2,1,0:T(8,128)(2,1)S(1)} collective-permute-done((bf16[4,576,128]{2,1,0:T(8,128)(2,1)S(1)}, bf16[4,576,128]{2,1,0:T(8,128)(2,1)S(1)}, u32[]{:S(2)}, u32[]{:S(2)}) %collective-permute-start.1) | collective-permute-done | bytes 589856 | tf_op jit(solution)/shard_map/ppermute | solution.py:46
  38.8 4.1 %shard_map.47 = (f32[4,256,768]{2,1,0:T(8,128)S(1)}, f32[4,256,768]{2,1,0:T(8,128)S(1)}) custom-call(s32[16,128]{1,0:T(8,128)S(1)} %get-tuple-element.12.seen_ref, bf16[4,256,640]{2,1,0:T(8,128)(2,1)S(1)} %get-tuple-element.13.own_ref.refs_0_.q_ref, ...), custom_call_target="tpu_custom_call", output_to_operand_aliasing={{0}: (3, {}), {1}: (4, {})} | custom-call | flops 4563402752 | bytes 4000000 | tf_op jit(solution)/shard_map/pallas_call | solution.py:291
  42.8 2.5 %collective-permute-done.2.refs_2_ = bf16[4,576,128]{2,1,0:T(8,128)(2,1)S(1)} collective-permute-done((bf16[4,576,128]{2,1,0:T(8,128)(2,1)S(1)}, bf16[4,576,128]{2,1,0:T(8,128)(2,1)S(1)}, u32[]{:S(2)}, u32[]{:S(2)}) %collective-permute-start.2) | collective-permute-done | bytes 589856 | tf_op jit(solution)/shard_map/ppermute | solution.py:46
  45.3 2.1 %shard_map.49.state_ref = f32[4,256,768]{2,1,0:T(8,128)S(1)} custom-call(s32[16,128]{1,0:T(8,128)S(1)} %get-tuple-element.12.seen_ref, bf16[4,256,640]{2,1,0:T(8,128)(2,1)S(1)} %get-tuple-element.14.refs_1_.refs_0_.q_ref, f32[4,256,768]{2,1,0:T(8,128)S(1)} %get-tuple-element.18.refs_1_, ...), custom_call_target="tpu_custom_call", output_to_operand_aliasing={{}: (2, {})} | custom-call | flops 2281701376 | bytes 4000000 | tf_op jit(solution)/shard_map/pallas_call | solution.py:291
  47.4 0.0 collective-permute-done.3.refs_0_.kv_ref
  47.4 2.2 %shard_map.50 = bf16[4,256,640]{2,1,0:T(8,128)(2,1)S(1)} custom-call(s32[16,128]{1,0:T(8,128)S(1)} %get-tuple-element.12.seen_ref, bf16[4,256,640]{2,1,0:T(8,128)(2,1)S(1)} %get-tuple-element.14.refs_1_.refs_0_.q_ref, f32[4,256,768]{2,1,0:T(8,128)S(1)} %shard_map.49.state_ref, bf16[4,576,128]{2,1,0:T(8,128)(2,1)S(1)} %collective-permute-done.3.refs_0_.kv_ref), custom_call_target="tpu_custom_call" | custom-call | flops 2281701376 | bytes 4000000 | tf_op jit(solution)/shard_map/pallas_call | solution.py:291
  49.6 12.3 %collective-permute-start.4 = (bf16[4,256,640]{2,1,0:T(8,128)(2,1)S(1)}, bf16[4,256,640]{2,1,0:T(8,128)(2,1)S(1)}, u32[]{:S(2)}, u32[]{:S(2)}) collective-permute-start(bf16[4,256,640]{2,1,0:T(8,128)(2,1)S(1)} %shard_map.50), channel_id=1, source_target_pairs={{0,16},{16,0},{1,17},{17,1},{2,18},{18,2},{3,19},{19,3},{4,20},{20... | collective-permute-start | bytes 3932168 | tf_op jit(solution)/shard_map/ppermute | solution.py:333
  61.9 2.1 %shard_map.48.state_ref = f32[4,256,768]{2,1,0:T(8,128)S(1)} custom-call(s32[16,128]{1,0:T(8,128)S(1)} %get-tuple-element.12.seen_ref, bf16[4,256,640]{2,1,0:T(8,128)(2,1)S(1)} %get-tuple-element.13.own_ref.refs_0_.q_ref, f32[4,256,768]{2,1,0:T(8,128)S(1)} %get-tuple-element.17.refs_1_, ...), custom_call_target="tpu_custom_call", output_to_operand_aliasing={{}: (2, {})} | custom-call | flops 2281701376 | bytes 4000000 | tf_op jit(solution)/shard_map/pallas_call | solution.py:291
  64.0 0.3 collective-permute-done.4.other_ref
  64.3 3.2 %shard_map.51 = bf16[256,4,512]{2,1,0:T(4,128)(2,1)} custom-call(s32[16,128]{1,0:T(8,128)S(1)} %get-tuple-element.12.seen_ref, bf16[4,256,640]{2,1,0:T(8,128)(2,1)S(1)} %get-tuple-element.13.own_ref.refs_0_.q_ref, f32[4,256,768]{2,1,0:T(8,128)S(1)} %shard_map.48.state_ref, bf16[4,256,640]{2,1,0:T(8,128)(2,1)S(1)} %collective-permute-done.4.other_ref, ...), custom_call_target="tpu_custom_call" | custom-call | flops 2281701376 | bytes 4000000 | tf_op jit(solution)/shard_map/pallas_call | solution.py:291
Async XLA Ops:
  0.1 1.2 %copy-start = (bf16[256,4,512]{2,1,0:T(4,128)(2,1)S(1)}, bf16[256,4,512]{2,1,0:T(4,128)(2,1)}, u32[]{:S(2)}) copy-start(bf16[256,4,512]{2,1,0:T(4,128)(2,1)} %latent_ref.1) | copy-start | bytes 3145732
  1.3 0.9 %copy-start.1 = (bf16[256,256]{1,0:T(8,128)(2,1)S(1)}, bf16[256,256]{1,0:T(8,128)(2,1)}, u32[]{:S(2)}) copy-start(bf16[256,256]{1,0:T(8,128)(2,1)} %rope_ref.1) | copy-start | bytes 393220
  2.2 0.7 copy-start.2
  5.9 28.5 %collective-permute-start = (bf16[4,256,640]{2,1,0:T(8,128)(2,1)S(1)}, bf16[4,256,640]{2,1,0:T(8,128)(2,1)S(1)}, u32[]{:S(2)}, u32[]{:S(2)}) collective-permute-start(bf16[4,256,640]{2,1,0:T(8,128)(2,1)S(1)} %get-tuple-element.13.own_ref.refs_0_.q_ref), channel_id=1, source_target_pairs={{0,16},{16,0},{1,17},{17,1},{2,18},{18,2},{3,19},{19,3},{4,20},{20... | collective-permute-start | bytes 3932168 | tf_op jit(solution)/shard_map/ppermute | solution.py:315
  26.0 12.8 %collective-permute-start.1 = (bf16[4,576,128]{2,1,0:T(8,128)(2,1)S(1)}, bf16[4,576,128]{2,1,0:T(8,128)(2,1)S(1)}, u32[]{:S(2)}, u32[]{:S(2)}) collective-permute-start(bf16[4,576,128]{2,1,0:T(8,128)(2,1)S(1)} %all_to_all.6.kv_ref), channel_id=1, source_target_pairs={{0,8},{4,12},{8,0},{12,4},{16,18},{20,22},{24,26},{28,30},{1,9},{5... | collective-permute-start | bytes 1769480 | tf_op jit(solution)/shard_map/ppermute | solution.py:46
  27.9 17.4 %collective-permute-start.2 = (bf16[4,576,128]{2,1,0:T(8,128)(2,1)S(1)}, bf16[4,576,128]{2,1,0:T(8,128)(2,1)S(1)}, u32[]{:S(2)}, u32[]{:S(2)}) collective-permute-start(bf16[4,576,128]{2,1,0:T(8,128)(2,1)S(1)} %all_to_all.6.kv_ref), channel_id=1, source_target_pairs={{0,4},{4,8},{8,12},{12,0},{16,17},{20,21},{24,25},{28,29},{1,5},{5... | collective-permute-start | bytes 1769480 | tf_op jit(solution)/shard_map/ppermute | solution.py:46
  30.2 17.2 %collective-permute-start.3 = (bf16[4,576,128]{2,1,0:T(8,128)(2,1)S(1)}, bf16[4,576,128]{2,1,0:T(8,128)(2,1)S(1)}, u32[]{:S(2)}, u32[]{:S(2)}) collective-permute-start(bf16[4,576,128]{2,1,0:T(8,128)(2,1)S(1)} %all_to_all.6.kv_ref), channel_id=1, source_target_pairs={{0,12},{4,0},{8,4},{12,8},{16,51},{20,55},{24,59},{28,63},{1,13},{... | collective-permute-start | bytes 1769480 | tf_op jit(solution)/shard_map/ppermute | solution.py:46
  49.6 14.7 %collective-permute-start.4 = (bf16[4,256,640]{2,1,0:T(8,128)(2,1)S(1)}, bf16[4,256,640]{2,1,0:T(8,128)(2,1)S(1)}, u32[]{:S(2)}, u32[]{:S(2)}) collective-permute-start(bf16[4,256,640]{2,1,0:T(8,128)(2,1)S(1)} %shard_map.50), channel_id=1, source_target_pairs={{0,16},{16,0},{1,17},{17,1},{2,18},{18,2},{3,19},{19,3},{4,20},{20... | collective-permute-start | bytes 3932168 | tf_op jit(solution)/shard_map/ppermute | solution.py:333

commit v3 on v2

--- a/solution.py
+++ b/solution.py
@@ -44,6 +44,10 @@
                 at = lambda u, v: (((u // 4) * 2 + core) * 4 + v) * 4 + u % 4
                 pairs.append((at(y, x), at(to_y, to_x)))
     return lax.ppermute(value, RING, pairs)
+
+
+def in_hbm(value):
+    return pltpu.with_memory_space_constraint(value, pltpu.HBM)
 
 
 def near_groups():
@@ -224,8 +228,8 @@
 
 
 def prepare_kernel(order_ref, place_ref, latent_ref, rope_ref, out, seen_ref):
+    out[:, :, :WIDTH] = jnp.swapaxes(latent_ref[...], 0, 1)
     for h in range(4):
-        out[h, :, :WIDTH] = latent_ref[:, h, :]
         rope = rope_ref[:, h * 64 : h * 64 + 64]
         out[h, :, WIDTH:] = jnp.concatenate([rope, jnp.zeros_like(rope)], axis=1)
 
@@ -259,25 +263,30 @@
     )(order, place, latent, rope)
 
 
-def spread_kernel(place_ref, cache_ref, out):
-    for i in range(4):
-        out[i] = cache_ref[...]
-
-
-def spread(cache, place):
+def spread_kernel(cache_ref, out, held, sems):
+    first = pl.multiple_of(lax.axis_index("co") * HALF, HALF)
+    load = pltpu.make_async_copy(cache_ref.at[:, pl.ds(first, HALF)], held, sems.at[0])
+    load.start()
+    load.wait()
+    stores = [pltpu.make_async_copy(held, out.at[i], sems.at[1 + i]) for i in range(4)]
+    for store in stores:
+        store.start()
+    for store in stores:
+        store.wait()
+
+
+def spread(cache):
     rows = cache.shape[0]
+    hbm = pl.BlockSpec(memory_space=pltpu.HBM)
     copies = pl.pallas_call(
         spread_kernel,
-        grid_spec=pltpu.PrefetchScalarGridSpec(
-            num_scalar_prefetch=1,
-            grid=(1,),
-            in_specs=[pl.BlockSpec((rows, HALF), lambda i, place: (0, place[0]))],
-            out_specs=pl.BlockSpec((4, rows, HALF), lambda i, place: (0, 0, 0)),
-        ),
+        in_specs=[hbm],
+        out_specs=hbm,
         out_shape=jax.ShapeDtypeStruct((4, rows, HALF), cache.dtype),
+        scratch_shapes=[pltpu.VMEM((rows, HALF), cache.dtype), pltpu.SemaphoreType.DMA((5,))],
         compiler_params=pltpu.CompilerParams(vmem_limit_bytes=VMEM_MIB * 2**20),
         name="spread",
-    )(place, cache)
+    )(cache)
     return copies.reshape(4 * rows, HALF)
 
 
@@ -305,9 +314,9 @@
     core = lax.axis_index("co")
     x, y = lax.axis_index("x"), lax.axis_index("yl")
     where = [group_order, jnp.stack([core, x, y]).astype(jnp.int32)]
-    copies = spread(pltpu.with_memory_space_constraint(latent_cache, pltpu.HBM), where[1])
+    copies = spread(in_hbm(latent_cache))
     bundle = lax.all_to_all(copies, RING, 0, 0, axis_index_groups=near_groups(), tiled=True)
-    queries, seen = prepare(*where, query_latent, query_rope)
+    queries, seen = prepare(*where, in_hbm(query_latent), in_hbm(query_rope))
     bundle = bundle.reshape(4, WIDTH + 64, HALF)
     far = []
     for shift in (1, -1, 2):

time: 68 us -> 65.4 us (0.962)
  local copies, waits for them, and re-layouts: 2.78 us -> 0.66 us
    unnamed x6 -> x2, local copies, waits for them, and re-layouts: 2.78 us -> 0.66 us
  transfers between devices with their start and end apart: 5 -> 5, of which waited for: 3 -> 3; matrix products, arithmetic and copies ran while one was open for 0% -> 0% of each run, Pallas kernels for 19% -> 20%
where the time goes in v3:
time: 65.4 us; the launch traced here: 65.1 us
  starting transfers between devices  29.4 us (45%)
  Pallas kernels  20.8 us (32%)
  blocking collectives  9.81 us (15%)
  waiting for transfers between devices  4.09 us (6%)
  local copies, waits for them, and re-layouts  0.66 us (1%)
    pallas_call x6, Pallas kernels, call(): pl.pallas_call(kernel, out_shape=out_shape, in_specs=[VM] * len(args), ou...  16.7 us
    ppermute x1, starting transfers between devices, attend(): other = lax.ppermute(sib, 'co', [(0, 1), (1, 0)])  12.2 us
    all_to_all x1, blocking collectives, attend(): lax.all_to_all(copies, RING, 0, 0, axis_index_groups=near_groups(), tiled...  9.81 us
    ppermute x1, starting transfers between devices, attend(): twin = lax.ppermute(queries, 'co', [(0, 1), (1, 0)])  8.75 us
    ppermute x3, starting transfers between devices, split_permute(): return lax.ppermute(value, RING, pairs)  8.4 us
    ppermute x3, waiting for transfers between devices, split_permute(): return lax.ppermute(value, RING, pairs)  3.75 us
    pallas_call x1, Pallas kernels, prepare(): pl.pallas_call(prepare_kernel, grid=(4,), out_shape=[jax.ShapeDtypeStruct...  2.4 us
    pallas_call x1, Pallas kernels, spread(): pl.pallas_call(spread_kernel, in_specs=[hbm], out_specs=hbm, out_shape=ja...  1.69 us
  transfers between devices with their start and end apart: 5, of which 3 were waited for; matrix products, arithmetic and copies ran while one was open for 0% of the time, Pallas kernels for 20%

profile of v3, /device:TPU:1, one launch (start us, length us, event | category | flops | bytes accessed | tf_op | source)
XLA Modules:
  0.0 65.1 jit_solution(2612722651656877824)
XLA Ops:
  0.0 0.1 pad_add_fusion.place_ref
  0.1 0.0 copy-start
  0.1 0.7 %copy-done = s32[16]{0:T(128)S(1)} copy-done((s32[16]{0:T(128)S(1)}, s32[16]{0:T(128)}, u32[]{:S(2)}) %copy-start) | copy-done | bytes 88
  0.7 2.4 %prepare.1 = (bf16[4,256,640]{2,1,0:T(8,128)(2,1)S(1)}, s32[16,128]{1,0:T(8,128)S(1)}) custom-call(s32[16]{0:T(128)S(1)} %copy-done, s32[3]{0:T(128)S(1)} %pad_add_fusion.place_ref, bf16[256,4,512]{2,1,0:T(4,128)(2,1)} %latent_ref.1, bf16[256,256]{1,0:T(8,128)(2,1)} %rope_ref.1), custom_call_target="tpu_custom_call" | custom-call | flops 1073741824 | bytes 2000000 | tf_op jit(solution)/shard_map/prepare/pallas_call | solution.py:243
  3.1 8.7 %collective-permute-start = (bf16[4,256,640]{2,1,0:T(8,128)(2,1)S(1)}, bf16[4,256,640]{2,1,0:T(8,128)(2,1)S(1)}, u32[]{:S(2)}, u32[]{:S(2)}) collective-permute-start(bf16[4,256,640]{2,1,0:T(8,128)(2,1)S(1)} %get-tuple-element.13.own_ref.refs_0_.q_ref), channel_id=1, source_target_pairs={{0,16},{16,0},{1,17},{17,1},{2,18},{18,2},{3,19},{19,3},{4,20},{20... | collective-permute-start | bytes 3932168 | tf_op jit(solution)/shard_map/ppermute | solution.py:324
  11.9 1.7 %spread.1 = bf16[4,576,128]{2,1,0:T(8,128)(2,1)S(1)} custom-call(bf16[576,256]{1,0:T(8,128)(2,1)} %cache_ref.1), custom_call_target="tpu_custom_call" | custom-call | tf_op jit(solution)/shard_map/spread/pallas_call | solution.py:281
  13.6 9.8 %all_to_all.6.kv_ref = bf16[4,576,128]{2,1,0:T(8,128)(2,1)S(1)} all-to-all(bf16[4,576,128]{2,1,0:T(8,128)(2,1)S(1)} %spread.1), channel_id=1, replica_groups={{0,1,2,3},{4,5,6,7},{8,9,10,11},{12,13,14,15},{16,20,24,28},{17,21,25,2..., dimensions={0} | all-to-all | bytes 1179648 | tf_op jit(solution)/shard_map/all_to_all | solution.py:318
  23.4 1.9 %collective-permute-start.1 = (bf16[4,576,128]{2,1,0:T(8,128)(2,1)S(1)}, bf16[4,576,128]{2,1,0:T(8,128)(2,1)S(1)}, u32[]{:S(2)}, u32[]{:S(2)}) collective-permute-start(bf16[4,576,128]{2,1,0:T(8,128)(2,1)S(1)} %all_to_all.6.kv_ref), channel_id=1, source_target_pairs={{0,8},{4,12},{8,0},{12,4},{16,18},{20,22},{24,26},{28,30},{1,9},{5... | collective-permute-start | bytes 1769480 | tf_op jit(solution)/shard_map/ppermute | solution.py:46
  25.3 2.4 %collective-permute-start.2 = (bf16[4,576,128]{2,1,0:T(8,128)(2,1)S(1)}, bf16[4,576,128]{2,1,0:T(8,128)(2,1)S(1)}, u32[]{:S(2)}, u32[]{:S(2)}) collective-permute-start(bf16[4,576,128]{2,1,0:T(8,128)(2,1)S(1)} %all_to_all.6.kv_ref), channel_id=1, source_target_pairs={{0,4},{4,8},{8,12},{12,0},{16,17},{20,21},{24,25},{28,29},{1,5},{5... | collective-permute-start | bytes 1769480 | tf_op jit(solution)/shard_map/ppermute | solution.py:46
  27.7 4.1 %collective-permute-start.3 = (bf16[4,576,128]{2,1,0:T(8,128)(2,1)S(1)}, bf16[4,576,128]{2,1,0:T(8,128)(2,1)S(1)}, u32[]{:S(2)}, u32[]{:S(2)}) collective-permute-start(bf16[4,576,128]{2,1,0:T(8,128)(2,1)S(1)} %all_to_all.6.kv_ref), channel_id=1, source_target_pairs={{0,12},{4,0},{8,4},{12,8},{16,51},{20,55},{24,59},{28,63},{1,13},{... | collective-permute-start | bytes 1769480 | tf_op jit(solution)/shard_map/ppermute | solution.py:46
  31.8 0.0 collective-permute-done.twin_ref
  31.8 3.1 %shard_map.46 = (f32[4,256,768]{2,1,0:T(8,128)S(1)}, f32[4,256,768]{2,1,0:T(8,128)S(1)}, bf16[4,256,640]{2,1,0:T(8,128)(2,1)S(1)}) custom-call(s32[16,128]{1,0:T(8,128)S(1)} %get-tuple-element.12.seen_ref, bf16[4,256,640]{2,1,0:T(8,128)(2,1)S(1)} %get-tuple-element.13.own_ref.refs_0_.q_ref, bf16[4,256,640]{2,1,0:T(8,128)(2,1)S(1)} %collective-permute-done.twin_ref, ...), custom_call_target="tpu_custom_call" | custom-call | flops 4563402752 | bytes 4000000 | tf_op jit(solution)/shard_map/pallas_call | solution.py:300
  34.9 1.3 %collective-permute-done.1.refs_4_ = bf16[4,576,128]{2,1,0:T(8,128)(2,1)S(1)} collective-permute-done((bf16[4,576,128]{2,1,0:T(8,128)(2,1)S(1)}, bf16[4,576,128]{2,1,0:T(8,128)(2,1)S(1)}, u32[]{:S(2)}, u32[]{:S(2)}) %collective-permute-start.1) | collective-permute-done | bytes 589856 | tf_op jit(solution)/shard_map/ppermute | solution.py:46
  36.2 4.0 %shard_map.47 = (f32[4,256,768]{2,1,0:T(8,128)S(1)}, f32[4,256,768]{2,1,0:T(8,128)S(1)}) custom-call(s32[16,128]{1,0:T(8,128)S(1)} %get-tuple-element.12.seen_ref, bf16[4,256,640]{2,1,0:T(8,128)(2,1)S(1)} %get-tuple-element.13.own_ref.refs_0_.q_ref, ...), custom_call_target="tpu_custom_call", output_to_operand_aliasing={{0}: (3, {}), {1}: (4, {})} | custom-call | flops 4563402752 | bytes 4000000 | tf_op jit(solution)/shard_map/pallas_call | solution.py:300
  40.3 2.5 %collective-permute-done.2.refs_2_ = bf16[4,576,128]{2,1,0:T(8,128)(2,1)S(1)} collective-permute-done((bf16[4,576,128]{2,1,0:T(8,128)(2,1)S(1)}, bf16[4,576,128]{2,1,0:T(8,128)(2,1)S(1)}, u32[]{:S(2)}, u32[]{:S(2)}) %collective-permute-start.2) | collective-permute-done | bytes 589856 | tf_op jit(solution)/shard_map/ppermute | solution.py:46
  42.7 2.1 %shard_map.49.state_ref = f32[4,256,768]{2,1,0:T(8,128)S(1)} custom-call(s32[16,128]{1,0:T(8,128)S(1)} %get-tuple-element.12.seen_ref, bf16[4,256,640]{2,1,0:T(8,128)(2,1)S(1)} %get-tuple-element.14.refs_1_.refs_0_.q_ref, f32[4,256,768]{2,1,0:T(8,128)S(1)} %get-tuple-element.18.refs_1_, ...), custom_call_target="tpu_custom_call", output_to_operand_aliasing={{}: (2, {})} | custom-call | flops 2281701376 | bytes 4000000 | tf_op jit(solution)/shard_map/pallas_call | solution.py:300
  44.9 0.0 collective-permute-done.3.refs_0_.kv_ref
  44.9 2.2 %shard_map.50 = bf16[4,256,640]{2,1,0:T(8,128)(2,1)S(1)} custom-call(s32[16,128]{1,0:T(8,128)S(1)} %get-tuple-element.12.seen_ref, bf16[4,256,640]{2,1,0:T(8,128)(2,1)S(1)} %get-tuple-element.14.refs_1_.refs_0_.q_ref, f32[4,256,768]{2,1,0:T(8,128)S(1)} %shard_map.49.state_ref, bf16[4,576,128]{2,1,0:T(8,128)(2,1)S(1)} %collective-permute-done.3.refs_0_.kv_ref), custom_call_target="tpu_custom_call" | custom-call | flops 2281701376 | bytes 4000000 | tf_op jit(solution)/shard_map/pallas_call | solution.py:300
  47.1 12.2 %collective-permute-start.4 = (bf16[4,256,640]{2,1,0:T(8,128)(2,1)S(1)}, bf16[4,256,640]{2,1,0:T(8,128)(2,1)S(1)}, u32[]{:S(2)}, u32[]{:S(2)}) collective-permute-start(bf16[4,256,640]{2,1,0:T(8,128)(2,1)S(1)} %shard_map.50), channel_id=1, source_target_pairs={{0,16},{16,0},{1,17},{17,1},{2,18},{18,2},{3,19},{19,3},{4,20},{20... | collective-permute-start | bytes 3932168 | tf_op jit(solution)/shard_map/ppermute | solution.py:342
  59.3 2.1 %shard_map.48.state_ref = f32[4,256,768]{2,1,0:T(8,128)S(1)} custom-call(s32[16,128]{1,0:T(8,128)S(1)} %get-tuple-element.12.seen_ref, bf16[4,256,640]{2,1,0:T(8,128)(2,1)S(1)} %get-tuple-element.13.own_ref.refs_0_.q_ref, f32[4,256,768]{2,1,0:T(8,128)S(1)} %get-tuple-element.17.refs_1_, ...), custom_call_target="tpu_custom_call", output_to_operand_aliasing={{}: (2, {})} | custom-call | flops 2281701376 | bytes 4000000 | tf_op jit(solution)/shard_map/pallas_call | solution.py:300
  61.4 0.3 collective-permute-done.4.other_ref
  61.8 3.2 %shard_map.51 = bf16[256,4,512]{2,1,0:T(4,128)(2,1)} custom-call(s32[16,128]{1,0:T(8,128)S(1)} %get-tuple-element.12.seen_ref, bf16[4,256,640]{2,1,0:T(8,128)(2,1)S(1)} %get-tuple-element.13.own_ref.refs_0_.q_ref, f32[4,256,768]{2,1,0:T(8,128)S(1)} %shard_map.48.state_ref, bf16[4,256,640]{2,1,0:T(8,128)(2,1)S(1)} %collective-permute-done.4.other_ref, ...), custom_call_target="tpu_custom_call" | custom-call | flops 2281701376 | bytes 4000000 | tf_op jit(solution)/shard_map/pallas_call | solution.py:300
Async XLA Ops:
  0.1 0.7 %copy-start = (s32[16]{0:T(128)S(1)}, s32[16]{0:T(128)}, u32[]{:S(2)}) copy-start(s32[16]{0:T(128)} %order_ref.1) | copy-start | bytes 196
  3.1 28.7 %collective-permute-start = (bf16[4,256,640]{2,1,0:T(8,128)(2,1)S(1)}, bf16[4,256,640]{2,1,0:T(8,128)(2,1)S(1)}, u32[]{:S(2)}, u32[]{:S(2)}) collective-permute-start(bf16[4,256,640]{2,1,0:T(8,128)(2,1)S(1)} %get-tuple-element.13.own_ref.refs_0_.q_ref), channel_id=1, source_target_pairs={{0,16},{16,0},{1,17},{17,1},{2,18},{18,2},{3,19},{19,3},{4,20},{20... | collective-permute-start | bytes 3932168 | tf_op jit(solution)/shard_map/ppermute | solution.py:324
  23.4 12.8 %collective-permute-start.1 = (bf16[4,576,128]{2,1,0:T(8,128)(2,1)S(1)}, bf16[4,576,128]{2,1,0:T(8,128)(2,1)S(1)}, u32[]{:S(2)}, u32[]{:S(2)}) collective-permute-start(bf16[4,576,128]{2,1,0:T(8,128)(2,1)S(1)} %all_to_all.6.kv_ref), channel_id=1, source_target_pairs={{0,8},{4,12},{8,0},{12,4},{16,18},{20,22},{24,26},{28,30},{1,9},{5... | collective-permute-start | bytes 1769480 | tf_op jit(solution)/shard_map/ppermute | solution.py:46
  25.3 17.4 %collective-permute-start.2 = (bf16[4,576,128]{2,1,0:T(8,128)(2,1)S(1)}, bf16[4,576,128]{2,1,0:T(8,128)(2,1)S(1)}, u32[]{:S(2)}, u32[]{:S(2)}) collective-permute-start(bf16[4,576,128]{2,1,0:T(8,128)(2,1)S(1)} %all_to_all.6.kv_ref), channel_id=1, source_target_pairs={{0,4},{4,8},{8,12},{12,0},{16,17},{20,21},{24,25},{28,29},{1,5},{5... | collective-permute-start | bytes 1769480 | tf_op jit(solution)/shard_map/ppermute | solution.py:46
  27.7 17.2 %collective-permute-start.3 = (bf16[4,576,128]{2,1,0:T(8,128)(2,1)S(1)}, bf16[4,576,128]{2,1,0:T(8,128)(2,1)S(1)}, u32[]{:S(2)}, u32[]{:S(2)}) collective-permute-start(bf16[4,576,128]{2,1,0:T(8,128)(2,1)S(1)} %all_to_all.6.kv_ref), channel_id=1, source_target_pairs={{0,12},{4,0},{8,4},{12,8},{16,51},{20,55},{24,59},{28,63},{1,13},{... | collective-permute-start | bytes 1769480 | tf_op jit(solution)/shard_map/ppermute | solution.py:46
  47.1 14.7 %collective-permute-start.4 = (bf16[4,256,640]{2,1,0:T(8,128)(2,1)S(1)}, bf16[4,256,640]{2,1,0:T(8,128)(2,1)S(1)}, u32[]{:S(2)}, u32[]{:S(2)}) collective-permute-start(bf16[4,256,640]{2,1,0:T(8,128)(2,1)S(1)} %shard_map.50), channel_id=1, source_target_pairs={{0,16},{16,0},{1,17},{17,1},{2,18},{18,2},{3,19},{19,3},{4,20},{20... | collective-permute-start | bytes 3932168 | tf_op jit(solution)/shard_map/ppermute | solution.py:342

commit v4 on v3

--- a/solution.py
+++ b/solution.py
@@ -129,8 +129,8 @@
     ref[h, :, TOTAL] = total
 
 
-def near_kernel(seen_ref, own_ref, twin_ref, kv_ref, own_out, sib_out, keep_ref):
-    keys = keys_of([kv_ref])
+def near_kernel(seen_ref, own_ref, twin_ref, kv_ref, far_ref, own_out, sib_out, keep_ref):
+    keys = keys_of([kv_ref, far_ref])
     rows = own_ref.shape[1]
     lane = lax.broadcasted_iota(jnp.int32, (rows, HALF), 1)
     ahead_by = lane - lax.broadcasted_iota(jnp.int32, (rows, HALF), 0)
@@ -142,8 +142,9 @@
             ahead = scores_of(work[i + 1][0][work[i + 1][2]], keys)
         parts = [
             jnp.where(ahead_by <= seen_ref[j : j + 1, :], part, MASKED)
-            for j, part in enumerate(pieces_of(scores))
+            for j, part in enumerate(pieces_of(scores[:, : 4 * HALF]))
         ]
+        parts += masked_pieces(scores[:, 4 * HALF :], seen_ref, (2,))
         floor = jnp.full((rows, HALF), FLOOR, f32)
         weights, peak, total, _ = soften(parts, floor, None)
         put_state(out, h, mix(weights, keys), peak, total)
@@ -333,9 +334,8 @@
         return call(kernel, [state] * count, 4 * len(parts) * count, args, aliases)
 
     packed = jax.ShapeDtypeStruct(twin.shape, twin.dtype)
-    args = [seen, queries, twin, bundle]
-    own, sib, twin = call(near_kernel, [state, state, packed], 8, args)
-    own, sib = more([queries, twin], [own, sib], 2)
+    args = [seen, queries, twin, bundle, far[2]]
+    own, sib, twin = call(near_kernel, [state, state, packed], 16, args)
     (sib,) = more([twin], [sib], 0)
     send = functools.partial(send_kernel, (1,))
     sib = call(send, packed, 4, [seen, twin, sib, far[1]])

time: 65.4 us -> 55.3 us (0.85)
  blocking collectives: 9.81 us -> 0 us
  starting transfers between devices: 29.4 us -> 31 us
  Pallas kernels: 20.8 us -> 19.7 us
    all_to_all x1 -> x0, blocking collectives: 9.81 us -> none  [attend(): lax.all_to_all(copies, RING, 0, 0, axis_index_groups=near_groups(), tiled...]
    all_to_all x0 -> x1, starting transfers between devices: none -> 4.84 us  [attend(): lax.all_to_all(copies, RING, 0, 0, axis_index_groups=near_groups(), tiled...]
    ppermute x1, starting transfers between devices: 12.2 us -> 8.95 us  [attend(): other = lax.ppermute(sib, 'co', [(0, 1), (1, 0)])]
    ppermute x3, starting transfers between devices: 8.4 us -> 9.79 us  [split_permute(): return lax.ppermute(value, RING, pairs)]
    ppermute x1, starting transfers between devices: 8.75 us -> 7.41 us  [attend(): twin = lax.ppermute(queries, 'co', [(0, 1), (1, 0)])]
    pallas_call x6 -> x5, Pallas kernels: 16.7 us -> 15.5 us  [call(): pl.pallas_call(kernel, out_shape=out_shape, in_specs=[VM] * len(args), ou...]
  transfers between devices with their start and end apart: 5 -> 6, of which waited for: 3 -> 3; matrix products, arithmetic and copies ran while one was open for 0% -> 0% of each run, Pallas kernels for 20% -> 23%
where the time goes in v4:
time: 55.3 us; the launch traced here: 55 us
  starting transfers between devices  31 us (56%)
  Pallas kernels  19.7 us (36%)
  waiting for transfers between devices  3.96 us (7%)
    pallas_call x5, Pallas kernels, call(): pl.pallas_call(kernel, out_shape=out_shape, in_specs=[VM] * len(args), ou...  15.5 us
    ppermute x3, starting transfers between devices, split_permute(): return lax.ppermute(value, RING, pairs)  9.79 us
    ppermute x1, starting transfers between devices, attend(): other = lax.ppermute(sib, 'co', [(0, 1), (1, 0)])  8.95 us
    ppermute x1, starting transfers between devices, attend(): twin = lax.ppermute(queries, 'co', [(0, 1), (1, 0)])  7.41 us
    all_to_all x1, starting transfers between devices, attend(): lax.all_to_all(copies, RING, 0, 0, axis_index_groups=near_groups(), tiled...  4.84 us
    ppermute x3, waiting for transfers between devices, split_permute(): return lax.ppermute(value, RING, pairs)  3.62 us
    pallas_call x1, Pallas kernels, prepare(): pl.pallas_call(prepare_kernel, grid=(4,), out_shape=[jax.ShapeDtypeStruct...  2.4 us
    pallas_call x1, Pallas kernels, spread(): pl.pallas_call(spread_kernel, in_specs=[hbm], out_specs=hbm, out_shape=ja...  1.77 us
  transfers between devices with their start and end apart: 6, of which 3 were waited for; matrix products, arithmetic and copies ran while one was open for 0% of the time, Pallas kernels for 23%

profile of v4, /device:TPU:1, one launch (start us, length us, event | category | flops | bytes accessed | tf_op | source)
XLA Modules:
  0.0 55.0 jit_solution(15036468905778671746)
XLA Ops:
  0.0 0.0 copy-start
  0.0 1.8 %spread.1 = bf16[4,576,128]{2,1,0:T(8,128)(2,1)} custom-call(bf16[576,256]{1,0:T(8,128)(2,1)} %cache_ref.1), custom_call_target="tpu_custom_call" | custom-call | tf_op jit(solution)/shard_map/spread/pallas_call | solution.py:282
  1.8 4.8 %all-to-all-start = ((bf16[4,576,128]{2,1,0:T(8,128)(2,1)}), bf16[4,576,128]{2,1,0:T(8,128)(2,1)S(1)}, u32[]{:S(2)}, u32[]{:S(2)}) async-start(bf16[4,576,128]{2,1,0:T(8,128)(2,1)} %spread.1), calls=%async_computation | async-start | bytes 1179648 | tf_op jit(solution)/shard_map/all_to_all | solution.py:319
  6.6 0.1 pad_add_fusion.place_ref
  6.7 0.0 copy-done
  6.7 2.4 %prepare.1 = (bf16[4,256,640]{2,1,0:T(8,128)(2,1)S(1)}, s32[16,128]{1,0:T(8,128)S(1)}) custom-call(s32[16]{0:T(128)S(1)} %copy-done, s32[3]{0:T(128)S(1)} %pad_add_fusion.place_ref, bf16[256,4,512]{2,1,0:T(4,128)(2,1)} %latent_ref.1, bf16[256,256]{1,0:T(8,128)(2,1)} %rope_ref.1), custom_call_target="tpu_custom_call" | custom-call | flops 1073741824 | bytes 2000000 | tf_op jit(solution)/shard_map/prepare/pallas_call | solution.py:244
  9.1 7.4 %collective-permute-start = (bf16[4,256,640]{2,1,0:T(8,128)(2,1)S(1)}, bf16[4,256,640]{2,1,0:T(8,128)(2,1)S(1)}, u32[]{:S(2)}, u32[]{:S(2)}) collective-permute-start(bf16[4,256,640]{2,1,0:T(8,128)(2,1)S(1)} %get-tuple-element.11.own_ref.refs_0_.q_ref), channel_id=1, source_target_pairs={{0,16},{16,0},{1,17},{17,1},{2,18},{18,2},{3,19},{19,3},{4,20},{20... | collective-permute-start | bytes 3932168 | tf_op jit(solution)/shard_map/ppermute | solution.py:325
  16.5 0.0 all-to-all-done.kv_ref
  16.5 4.5 %collective-permute-start.1 = (bf16[4,576,128]{2,1,0:T(8,128)(2,1)S(1)}, bf16[4,576,128]{2,1,0:T(8,128)(2,1)S(1)}, u32[]{:S(2)}, u32[]{:S(2)}) collective-permute-start(bf16[4,576,128]{2,1,0:T(8,128)(2,1)S(1)} %all-to-all-done.kv_ref), channel_id=1, source_target_pairs={{0,8},{4,12},{8,0},{12,4},{16,18},{20,22},{24,26},{28,30},{1,9},{5... | collective-permute-start | bytes 1769480 | tf_op jit(solution)/shard_map/ppermute | solution.py:46
  21.1 1.9 %collective-permute-start.3 = (bf16[4,576,128]{2,1,0:T(8,128)(2,1)S(1)}, bf16[4,576,128]{2,1,0:T(8,128)(2,1)S(1)}, u32[]{:S(2)}, u32[]{:S(2)}) collective-permute-start(bf16[4,576,128]{2,1,0:T(8,128)(2,1)S(1)} %all-to-all-done.kv_ref), channel_id=1, source_target_pairs={{0,12},{4,0},{8,4},{12,8},{16,51},{20,55},{24,59},{28,63},{1,13},{... | collective-permute-start | bytes 1769480 | tf_op jit(solution)/shard_map/ppermute | solution.py:46
  23.0 3.4 %collective-permute-start.2 = (bf16[4,576,128]{2,1,0:T(8,128)(2,1)S(1)}, bf16[4,576,128]{2,1,0:T(8,128)(2,1)S(1)}, u32[]{:S(2)}, u32[]{:S(2)}) collective-permute-start(bf16[4,576,128]{2,1,0:T(8,128)(2,1)S(1)} %all-to-all-done.kv_ref), channel_id=1, source_target_pairs={{0,4},{4,8},{8,12},{12,0},{16,17},{20,21},{24,25},{28,29},{1,5},{5... | collective-permute-start | bytes 1769480 | tf_op jit(solution)/shard_map/ppermute | solution.py:46
  26.4 0.0 collective-permute-done.twin_ref
  26.4 3.0 %collective-permute-done.1.far_ref = bf16[4,576,128]{2,1,0:T(8,128)(2,1)S(1)} collective-permute-done((bf16[4,576,128]{2,1,0:T(8,128)(2,1)S(1)}, bf16[4,576,128]{2,1,0:T(8,128)(2,1)S(1)}, u32[]{:S(2)}, u32[]{:S(2)}) %collective-permute-start.1) | collective-permute-done | bytes 589856 | tf_op jit(solution)/shard_map/ppermute | solution.py:46
  29.4 5.9 %shard_map.46 = (f32[4,256,768]{2,1,0:T(8,128)S(1)}, f32[4,256,768]{2,1,0:T(8,128)S(1)}, bf16[4,256,640]{2,1,0:T(8,128)(2,1)S(1)}) custom-call(s32[16,128]{1,0:T(8,128)S(1)} %get-tuple-element.10.seen_ref, bf16[4,256,640]{2,1,0:T(8,128)(2,1)S(1)} %get-tuple-element.11.own_ref.refs_0_.q_ref, bf16[4,256,640]{2,1,0:T(8,128)(2,1)S(1)} %collective-permute-done.twin_ref, ...), custom_call_target="tpu_custom_call" | custom-call | flops 9126805504 | bytes 4000000 | tf_op jit(solution)/shard_map/pallas_call | solution.py:301
  35.3 0.6 %collective-permute-done.2.refs_2_ = bf16[4,576,128]{2,1,0:T(8,128)(2,1)S(1)} collective-permute-done((bf16[4,576,128]{2,1,0:T(8,128)(2,1)S(1)}, bf16[4,576,128]{2,1,0:T(8,128)(2,1)S(1)}, u32[]{:S(2)}, u32[]{:S(2)}) %collective-permute-start.2) | collective-permute-done | bytes 589856 | tf_op jit(solution)/shard_map/ppermute | solution.py:46
  35.9 2.1 %shard_map.48.state_ref = f32[4,256,768]{2,1,0:T(8,128)S(1)} custom-call(s32[16,128]{1,0:T(8,128)S(1)} %get-tuple-element.10.seen_ref, bf16[4,256,640]{2,1,0:T(8,128)(2,1)S(1)} %get-tuple-element.13.refs_0_.q_ref, f32[4,256,768]{2,1,0:T(8,128)S(1)} %get-tuple-element.14.refs_1_, ...), custom_call_target="tpu_custom_call", output_to_operand_aliasing={{}: (2, {})} | custom-call | flops 2281701376 | bytes 4000000 | tf_op jit(solution)/shard_map/pallas_call | solution.py:301
  38.0 0.0 collective-permute-done.3.refs_0_.kv_ref
  38.0 2.2 %shard_map.49 = bf16[4,256,640]{2,1,0:T(8,128)(2,1)S(1)} custom-call(s32[16,128]{1,0:T(8,128)S(1)} %get-tuple-element.10.seen_ref, bf16[4,256,640]{2,1,0:T(8,128)(2,1)S(1)} %get-tuple-element.13.refs_0_.q_ref, f32[4,256,768]{2,1,0:T(8,128)S(1)} %shard_map.48.state_ref, bf16[4,576,128]{2,1,0:T(8,128)(2,1)S(1)} %collective-permute-done.3.refs_0_.kv_ref), custom_call_target="tpu_custom_call" | custom-call | flops 2281701376 | bytes 4000000 | tf_op jit(solution)/shard_map/pallas_call | solution.py:301
  40.2 9.0 %collective-permute-start.4 = (bf16[4,256,640]{2,1,0:T(8,128)(2,1)S(1)}, bf16[4,256,640]{2,1,0:T(8,128)(2,1)S(1)}, u32[]{:S(2)}, u32[]{:S(2)}) collective-permute-start(bf16[4,256,640]{2,1,0:T(8,128)(2,1)S(1)} %shard_map.49), channel_id=1, source_target_pairs={{0,16},{16,0},{1,17},{17,1},{2,18},{18,2},{3,19},{19,3},{4,20},{20... | collective-permute-start | bytes 3932168 | tf_op jit(solution)/shard_map/ppermute | solution.py:342
  49.2 2.1 %shard_map.47.state_ref = f32[4,256,768]{2,1,0:T(8,128)S(1)} custom-call(s32[16,128]{1,0:T(8,128)S(1)} %get-tuple-element.10.seen_ref, bf16[4,256,640]{2,1,0:T(8,128)(2,1)S(1)} %get-tuple-element.11.own_ref.refs_0_.q_ref, f32[4,256,768]{2,1,0:T(8,128)S(1)} %get-tuple-element.12.refs_1_, ...), custom_call_target="tpu_custom_call", output_to_operand_aliasing={{}: (2, {})} | custom-call | flops 2281701376 | bytes 4000000 | tf_op jit(solution)/shard_map/pallas_call | solution.py:301
  51.3 0.3 collective-permute-done.4.other_ref
  51.6 3.2 %shard_map.50 = bf16[256,4,512]{2,1,0:T(4,128)(2,1)} custom-call(s32[16,128]{1,0:T(8,128)S(1)} %get-tuple-element.10.seen_ref, bf16[4,256,640]{2,1,0:T(8,128)(2,1)S(1)} %get-tuple-element.11.own_ref.refs_0_.q_ref, f32[4,256,768]{2,1,0:T(8,128)S(1)} %shard_map.47.state_ref, bf16[4,256,640]{2,1,0:T(8,128)(2,1)S(1)} %collective-permute-done.4.other_ref, ...), custom_call_target="tpu_custom_call" | custom-call | flops 2281701376 | bytes 4000000 | tf_op jit(solution)/shard_map/pallas_call | solution.py:301
Async XLA Ops:
  0.0 6.7 %copy-start = (s32[16]{0:T(128)S(1)}, s32[16]{0:T(128)}, u32[]{:S(2)}) copy-start(s32[16]{0:T(128)} %order_ref.1) | copy-start | bytes 196
  1.8 14.8 %all-to-all-start = ((bf16[4,576,128]{2,1,0:T(8,128)(2,1)}), bf16[4,576,128]{2,1,0:T(8,128)(2,1)S(1)}, u32[]{:S(2)}, u32[]{:S(2)}) async-start(bf16[4,576,128]{2,1,0:T(8,128)(2,1)} %spread.1), calls=%async_computation | async-start | bytes 1179648 | tf_op jit(solution)/shard_map/all_to_all | solution.py:319
  9.1 17.2 %collective-permute-start = (bf16[4,256,640]{2,1,0:T(8,128)(2,1)S(1)}, bf16[4,256,640]{2,1,0:T(8,128)(2,1)S(1)}, u32[]{:S(2)}, u32[]{:S(2)}) collective-permute-start(bf16[4,256,640]{2,1,0:T(8,128)(2,1)S(1)} %get-tuple-element.11.own_ref.refs_0_.q_ref), channel_id=1, source_target_pairs={{0,16},{16,0},{1,17},{17,1},{2,18},{18,2},{3,19},{19,3},{4,20},{20... | collective-permute-start | bytes 3932168 | tf_op jit(solution)/shard_map/ppermute | solution.py:325
  16.5 12.8 %collective-permute-start.1 = (bf16[4,576,128]{2,1,0:T(8,128)(2,1)S(1)}, bf16[4,576,128]{2,1,0:T(8,128)(2,1)S(1)}, u32[]{:S(2)}, u32[]{:S(2)}) collective-permute-start(bf16[4,576,128]{2,1,0:T(8,128)(2,1)S(1)} %all-to-all-done.kv_ref), channel_id=1, source_target_pairs={{0,8},{4,12},{8,0},{12,4},{16,18},{20,22},{24,26},{28,30},{1,9},{5... | collective-permute-start | bytes 1769480 | tf_op jit(solution)/shard_map/ppermute | solution.py:46
  21.1 17.0 %collective-permute-start.3 = (bf16[4,576,128]{2,1,0:T(8,128)(2,1)S(1)}, bf16[4,576,128]{2,1,0:T(8,128)(2,1)S(1)}, u32[]{:S(2)}, u32[]{:S(2)}) collective-permute-start(bf16[4,576,128]{2,1,0:T(8,128)(2,1)S(1)} %all-to-all-done.kv_ref), channel_id=1, source_target_pairs={{0,12},{4,0},{8,4},{12,8},{16,51},{20,55},{24,59},{28,63},{1,13},{... | collective-permute-start | bytes 1769480 | tf_op jit(solution)/shard_map/ppermute | solution.py:46
  23.0 12.9 %collective-permute-start.2 = (bf16[4,576,128]{2,1,0:T(8,128)(2,1)S(1)}, bf16[4,576,128]{2,1,0:T(8,128)(2,1)S(1)}, u32[]{:S(2)}, u32[]{:S(2)}) collective-permute-start(bf16[4,576,128]{2,1,0:T(8,128)(2,1)S(1)} %all-to-all-done.kv_ref), channel_id=1, source_target_pairs={{0,4},{4,8},{8,12},{12,0},{16,17},{20,21},{24,25},{28,29},{1,5},{5... | collective-permute-start | bytes 1769480 | tf_op jit(solution)/shard_map/ppermute | solution.py:46
  40.2 11.4 %collective-permute-start.4 = (bf16[4,256,640]{2,1,0:T(8,128)(2,1)S(1)}, bf16[4,256,640]{2,1,0:T(8,128)(2,1)S(1)}, u32[]{:S(2)}, u32[]{:S(2)}) collective-permute-start(bf16[4,256,640]{2,1,0:T(8,128)(2,1)S(1)} %shard_map.49), channel_id=1, source_target_pairs={{0,16},{16,0},{1,17},{17,1},{2,18},{18,2},{3,19},{19,3},{4,20},{20... | collective-permute-start | bytes 3932168 | tf_op jit(solution)/shard_map/ppermute | solution.py:342

commit v5 on v4

--- a/solution.py
+++ b/solution.py
@@ -336,9 +336,8 @@
     packed = jax.ShapeDtypeStruct(twin.shape, twin.dtype)
     args = [seen, queries, twin, bundle, far[2]]
     own, sib, twin = call(near_kernel, [state, state, packed], 16, args)
-    (sib,) = more([twin], [sib], 0)
-    send = functools.partial(send_kernel, (1,))
-    sib = call(send, packed, 4, [seen, twin, sib, far[1]])
+    send = functools.partial(send_kernel, (0, 1))
+    sib = call(send, packed, 8, [seen, twin, sib, far[0], far[1]])
     other = lax.ppermute(sib, "co", [(0, 1), (1, 0)])
     (own,) = more([queries], [own], 0)
     out = jax.ShapeDtypeStruct((rows, heads, WIDTH), jnp.bfloat16)

time: 55.3 us -> 54.8 us (level)
  waiting for transfers between devices: 3.96 us -> 2.75 us
  starting transfers between devices: 31 us -> 32.2 us
    ppermute x3, waiting for transfers between devices: 3.62 us -> 2.41 us  [split_permute(): return lax.ppermute(value, RING, pairs)]
    ppermute x3, starting transfers between devices: 9.79 us -> 11 us  [split_permute(): return lax.ppermute(value, RING, pairs)]
    pallas_call x5 -> x4, Pallas kernels: 15.5 us -> 15 us  [call(): pl.pallas_call(kernel, out_shape=out_shape, in_specs=[VM] * len(args), ou...]
  transfers between devices with their start and end apart: 6 -> 6, of which waited for: 3 -> 3; matrix products, arithmetic and copies ran while one was open for 0% -> 0% of each run, Pallas kernels for 23% -> 19%
where the time goes in v5:
time: 54.8 us; the launch traced here: 54.5 us
  starting transfers between devices  32.2 us (59%)
  Pallas kernels  19.2 us (35%)
  waiting for transfers between devices  2.75 us (5%)
    pallas_call x4, Pallas kernels, call(): pl.pallas_call(kernel, out_shape=out_shape, in_specs=[VM] * len(args), ou...  15 us
    ppermute x3, starting transfers between devices, split_permute(): return lax.ppermute(value, RING, pairs)  11 us
    ppermute x1, starting transfers between devices, attend(): other = lax.ppermute(sib, 'co', [(0, 1), (1, 0)])  8.95 us
    ppermute x1, starting transfers between devices, attend(): twin = lax.ppermute(queries, 'co', [(0, 1), (1, 0)])  7.41 us
    all_to_all x1, starting transfers between devices, attend(): lax.all_to_all(copies, RING, 0, 0, axis_index_groups=near_groups(), tiled...  4.84 us
    ppermute x3, waiting for transfers between devices, split_permute(): return lax.ppermute(value, RING, pairs)  2.41 us
    pallas_call x1, Pallas kernels, prepare(): pl.pallas_call(prepare_kernel, grid=(4,), out_shape=[jax.ShapeDtypeStruct...  2.4 us
    pallas_call x1, Pallas kernels, spread(): pl.pallas_call(spread_kernel, in_specs=[hbm], out_specs=hbm, out_shape=ja...  1.77 us
  transfers between devices with their start and end apart: 6, of which 3 were waited for; matrix products, arithmetic and copies ran while one was open for 0% of the time, Pallas kernels for 19%

profile of v5, /device:TPU:1, one launch (start us, length us, event | category | flops | bytes accessed | tf_op | source)
XLA Modules:
  0.0 54.5 jit_solution(13753353740563295478)
XLA Ops:
  0.0 0.0 copy-start
  0.0 1.8 %spread.1 = bf16[4,576,128]{2,1,0:T(8,128)(2,1)} custom-call(bf16[576,256]{1,0:T(8,128)(2,1)} %cache_ref.1), custom_call_target="tpu_custom_call" | custom-call | tf_op jit(solution)/shard_map/spread/pallas_call | solution.py:282
  1.8 4.8 %all-to-all-start = ((bf16[4,576,128]{2,1,0:T(8,128)(2,1)}), bf16[4,576,128]{2,1,0:T(8,128)(2,1)S(1)}, u32[]{:S(2)}, u32[]{:S(2)}) async-start(bf16[4,576,128]{2,1,0:T(8,128)(2,1)} %spread.1), calls=%async_computation | async-start | bytes 1179648 | tf_op jit(solution)/shard_map/all_to_all | solution.py:319
  6.6 0.1 pad_add_fusion.place_ref
  6.7 0.0 copy-done
  6.7 2.4 %prepare.1 = (bf16[4,256,640]{2,1,0:T(8,128)(2,1)S(1)}, s32[16,128]{1,0:T(8,128)S(1)}) custom-call(s32[16]{0:T(128)S(1)} %copy-done, s32[3]{0:T(128)S(1)} %pad_add_fusion.place_ref, bf16[256,4,512]{2,1,0:T(4,128)(2,1)} %latent_ref.1, bf16[256,256]{1,0:T(8,128)(2,1)} %rope_ref.1), custom_call_target="tpu_custom_call" | custom-call | flops 1073741824 | bytes 2000000 | tf_op jit(solution)/shard_map/prepare/pallas_call | solution.py:244
  9.1 7.4 %collective-permute-start = (bf16[4,256,640]{2,1,0:T(8,128)(2,1)S(1)}, bf16[4,256,640]{2,1,0:T(8,128)(2,1)S(1)}, u32[]{:S(2)}, u32[]{:S(2)}) collective-permute-start(bf16[4,256,640]{2,1,0:T(8,128)(2,1)S(1)} %get-tuple-element.11.own_ref.refs_0_.q_ref), channel_id=1, source_target_pairs={{0,16},{16,0},{1,17},{17,1},{2,18},{18,2},{3,19},{19,3},{4,20},{20... | collective-permute-start | bytes 3932168 | tf_op jit(solution)/shard_map/ppermute | solution.py:325
  16.5 0.0 all-to-all-done.kv_ref
  16.5 4.5 %collective-permute-start.1 = (bf16[4,576,128]{2,1,0:T(8,128)(2,1)S(1)}, bf16[4,576,128]{2,1,0:T(8,128)(2,1)S(1)}, u32[]{:S(2)}, u32[]{:S(2)}) collective-permute-start(bf16[4,576,128]{2,1,0:T(8,128)(2,1)S(1)} %all-to-all-done.kv_ref), channel_id=1, source_target_pairs={{0,8},{4,12},{8,0},{12,4},{16,18},{20,22},{24,26},{28,30},{1,9},{5... | collective-permute-start | bytes 1769480 | tf_op jit(solution)/shard_map/ppermute | solution.py:46
  21.1 1.9 %collective-permute-start.2 = (bf16[4,576,128]{2,1,0:T(8,128)(2,1)S(1)}, bf16[4,576,128]{2,1,0:T(8,128)(2,1)S(1)}, u32[]{:S(2)}, u32[]{:S(2)}) collective-permute-start(bf16[4,576,128]{2,1,0:T(8,128)(2,1)S(1)} %all-to-all-done.kv_ref), channel_id=1, source_target_pairs={{0,4},{4,8},{8,12},{12,0},{16,17},{20,21},{24,25},{28,29},{1,5},{5... | collective-permute-start | bytes 1769480 | tf_op jit(solution)/shard_map/ppermute | solution.py:46
  23.0 4.6 %collective-permute-start.3 = (bf16[4,576,128]{2,1,0:T(8,128)(2,1)S(1)}, bf16[4,576,128]{2,1,0:T(8,128)(2,1)S(1)}, u32[]{:S(2)}, u32[]{:S(2)}) collective-permute-start(bf16[4,576,128]{2,1,0:T(8,128)(2,1)S(1)} %all-to-all-done.kv_ref), channel_id=1, source_target_pairs={{0,12},{4,0},{8,4},{12,8},{16,51},{20,55},{24,59},{28,63},{1,13},{... | collective-permute-start | bytes 1769480 | tf_op jit(solution)/shard_map/ppermute | solution.py:46
  27.6 0.0 collective-permute-done.twin_ref
  27.6 1.8 %collective-permute-done.1.far_ref = bf16[4,576,128]{2,1,0:T(8,128)(2,1)S(1)} collective-permute-done((bf16[4,576,128]{2,1,0:T(8,128)(2,1)S(1)}, bf16[4,576,128]{2,1,0:T(8,128)(2,1)S(1)}, u32[]{:S(2)}, u32[]{:S(2)}) %collective-permute-start.1) | collective-permute-done | bytes 589856 | tf_op jit(solution)/shard_map/ppermute | solution.py:46
  29.4 5.9 %shard_map.46 = (f32[4,256,768]{2,1,0:T(8,128)S(1)}, f32[4,256,768]{2,1,0:T(8,128)S(1)}, bf16[4,256,640]{2,1,0:T(8,128)(2,1)S(1)}) custom-call(s32[16,128]{1,0:T(8,128)S(1)} %get-tuple-element.10.seen_ref, bf16[4,256,640]{2,1,0:T(8,128)(2,1)S(1)} %get-tuple-element.11.own_ref.refs_0_.q_ref, bf16[4,256,640]{2,1,0:T(8,128)(2,1)S(1)} %collective-permute-done.twin_ref, ...), custom_call_target="tpu_custom_call" | custom-call | flops 9126805504 | bytes 4000000 | tf_op jit(solution)/shard_map/pallas_call | solution.py:301
  35.3 0.6 %collective-permute-done.2.refs_2_.refs_0_ = bf16[4,576,128]{2,1,0:T(8,128)(2,1)S(1)} collective-permute-done((bf16[4,576,128]{2,1,0:T(8,128)(2,1)S(1)}, bf16[4,576,128]{2,1,0:T(8,128)(2,1)S(1)}, u32[]{:S(2)}, u32[]{:S(2)}) %collective-permute-start.2) | collective-permute-done | bytes 589856 | tf_op jit(solution)/shard_map/ppermute | solution.py:46
  35.9 0.0 collective-permute-done.3.refs_1_.kv_ref
  35.9 3.8 %shard_map.48 = bf16[4,256,640]{2,1,0:T(8,128)(2,1)S(1)} custom-call(s32[16,128]{1,0:T(8,128)S(1)} %get-tuple-element.10.seen_ref, bf16[4,256,640]{2,1,0:T(8,128)(2,1)S(1)} %get-tuple-element.13.q_ref, f32[4,256,768]{2,1,0:T(8,128)S(1)} %get-tuple-element.14.state_ref, bf16[4,576,128]{2,1,0:T(8,128)(2,1)S(1)} %collective-permute-done.2.refs_2_.refs_0_, ...), custom_call_target="tpu_custom_call" | custom-call | flops 4563402752 | bytes 4000000 | tf_op jit(solution)/shard_map/pallas_call | solution.py:301
  39.7 9.0 %collective-permute-start.4 = (bf16[4,256,640]{2,1,0:T(8,128)(2,1)S(1)}, bf16[4,256,640]{2,1,0:T(8,128)(2,1)S(1)}, u32[]{:S(2)}, u32[]{:S(2)}) collective-permute-start(bf16[4,256,640]{2,1,0:T(8,128)(2,1)S(1)} %shard_map.48), channel_id=1, source_target_pairs={{0,16},{16,0},{1,17},{17,1},{2,18},{18,2},{3,19},{19,3},{4,20},{20... | collective-permute-start | bytes 3932168 | tf_op jit(solution)/shard_map/ppermute | solution.py:341
  48.7 2.1 %shard_map.47.state_ref = f32[4,256,768]{2,1,0:T(8,128)S(1)} custom-call(s32[16,128]{1,0:T(8,128)S(1)} %get-tuple-element.10.seen_ref, bf16[4,256,640]{2,1,0:T(8,128)(2,1)S(1)} %get-tuple-element.11.own_ref.refs_0_.q_ref, f32[4,256,768]{2,1,0:T(8,128)S(1)} %get-tuple-element.12.refs_1_, ...), custom_call_target="tpu_custom_call", output_to_operand_aliasing={{}: (2, {})} | custom-call | flops 2281701376 | bytes 4000000 | tf_op jit(solution)/shard_map/pallas_call | solution.py:301
  50.8 0.3 collective-permute-done.4.other_ref
  51.1 3.2 %shard_map.49 = bf16[256,4,512]{2,1,0:T(4,128)(2,1)} custom-call(s32[16,128]{1,0:T(8,128)S(1)} %get-tuple-element.10.seen_ref, bf16[4,256,640]{2,1,0:T(8,128)(2,1)S(1)} %get-tuple-element.11.own_ref.refs_0_.q_ref, f32[4,256,768]{2,1,0:T(8,128)S(1)} %shard_map.47.state_ref, bf16[4,256,640]{2,1,0:T(8,128)(2,1)S(1)} %collective-permute-done.4.other_ref, ...), custom_call_target="tpu_custom_call" | custom-call | flops 2281701376 | bytes 4000000 | tf_op jit(solution)/shard_map/pallas_call | solution.py:301
Async XLA Ops:
  0.0 6.7 %copy-start = (s32[16]{0:T(128)S(1)}, s32[16]{0:T(128)}, u32[]{:S(2)}) copy-start(s32[16]{0:T(128)} %order_ref.1) | copy-start | bytes 196
  1.8 14.8 %all-to-all-start = ((bf16[4,576,128]{2,1,0:T(8,128)(2,1)}), bf16[4,576,128]{2,1,0:T(8,128)(2,1)S(1)}, u32[]{:S(2)}, u32[]{:S(2)}) async-start(bf16[4,576,128]{2,1,0:T(8,128)(2,1)} %spread.1), calls=%async_computation | async-start | bytes 1179648 | tf_op jit(solution)/shard_map/all_to_all | solution.py:319
  9.1 18.5 %collective-permute-start = (bf16[4,256,640]{2,1,0:T(8,128)(2,1)S(1)}, bf16[4,256,640]{2,1,0:T(8,128)(2,1)S(1)}, u32[]{:S(2)}, u32[]{:S(2)}) collective-permute-start(bf16[4,256,640]{2,1,0:T(8,128)(2,1)S(1)} %get-tuple-element.11.own_ref.refs_0_.q_ref), channel_id=1, source_target_pairs={{0,16},{16,0},{1,17},{17,1},{2,18},{18,2},{3,19},{19,3},{4,20},{20... | collective-permute-start | bytes 3932168 | tf_op jit(solution)/shard_map/ppermute | solution.py:325
  16.5 12.8 %collective-permute-start.1 = (bf16[4,576,128]{2,1,0:T(8,128)(2,1)S(1)}, bf16[4,576,128]{2,1,0:T(8,128)(2,1)S(1)}, u32[]{:S(2)}, u32[]{:S(2)}) collective-permute-start(bf16[4,576,128]{2,1,0:T(8,128)(2,1)S(1)} %all-to-all-done.kv_ref), channel_id=1, source_target_pairs={{0,8},{4,12},{8,0},{12,4},{16,18},{20,22},{24,26},{28,30},{1,9},{5... | collective-permute-start | bytes 1769480 | tf_op jit(solution)/shard_map/ppermute | solution.py:46
  21.1 14.8 %collective-permute-start.2 = (bf16[4,576,128]{2,1,0:T(8,128)(2,1)S(1)}, bf16[4,576,128]{2,1,0:T(8,128)(2,1)S(1)}, u32[]{:S(2)}, u32[]{:S(2)}) collective-permute-start(bf16[4,576,128]{2,1,0:T(8,128)(2,1)S(1)} %all-to-all-done.kv_ref), channel_id=1, source_target_pairs={{0,4},{4,8},{8,12},{12,0},{16,17},{20,21},{24,25},{28,29},{1,5},{5... | collective-permute-start | bytes 1769480 | tf_op jit(solution)/shard_map/ppermute | solution.py:46
  23.0 12.9 %collective-permute-start.3 = (bf16[4,576,128]{2,1,0:T(8,128)(2,1)S(1)}, bf16[4,576,128]{2,1,0:T(8,128)(2,1)S(1)}, u32[]{:S(2)}, u32[]{:S(2)}) collective-permute-start(bf16[4,576,128]{2,1,0:T(8,128)(2,1)S(1)} %all-to-all-done.kv_ref), channel_id=1, source_target_pairs={{0,12},{4,0},{8,4},{12,8},{16,51},{20,55},{24,59},{28,63},{1,13},{... | collective-permute-start | bytes 1769480 | tf_op jit(solution)/shard_map/ppermute | solution.py:46
  39.7 11.4 %collective-permute-start.4 = (bf16[4,256,640]{2,1,0:T(8,128)(2,1)S(1)}, bf16[4,256,640]{2,1,0:T(8,128)(2,1)S(1)}, u32[]{:S(2)}, u32[]{:S(2)}) collective-permute-start(bf16[4,256,640]{2,1,0:T(8,128)(2,1)S(1)} %shard_map.48), channel_id=1, source_target_pairs={{0,16},{16,0},{1,17},{17,1},{2,18},{18,2},{3,19},{19,3},{4,20},{20... | collective-permute-start | bytes 3932168 | tf_op jit(solution)/shard_map/ppermute | solution.py:341
